TPU v7x, 32 devices: a whole 2x2x4 slice. The times are simulated.
32 devices in a mesh: groups: 2 (over y), gx: 4 (over z), gy: 2 (over x), gz: 2 (over core).
Axes of the slice: x: 2, y: 2, z: 4, core: 2. Of those that a mesh axis runs over, the one named last changes fastest.
Arguments:
- coords: float32 [8, 8, 16, 3, 128], P(('groups', 'gx'), 'gy', 'gz'), parts along dimension 0, may hold values from 0 to 1.1
- charges: float32 [8, 8, 16, 128], P(('groups', 'gx'), 'gy', 'gz'), parts along dimension 0, may hold values from -2 to 2
- atom_types: int32 [8, 8, 16, 128], P(('groups', 'gx'), 'gy', 'gz'), parts along dimension 0, may hold values from 0 to 63
- counts: int32 [8, 8, 16], P(('groups', 'gx'), 'gy', 'gz'), parts along dimension 0, may hold values from 64 to 128
- c6_table: float32 [64, 64], replicated, may hold values from 0.0001 to 0.001
- c12_table: float32 [64, 64], replicated, may hold values from 1e-08 to 1e-07
Outputs:
- forces: float32 [8, 8, 16, 3, 128], P(('groups', 'gx'), 'gy', 'gz'), parts along dimension 0
- energy: float32 [2], P('groups'), parts along dimension 0
There are 2 independent parts, one for each index of `groups`. A program takes and returns all parts, laid end to end along the dimension named above; an argument that names none is the same for every part. Nothing has to cross between parts.
All inputs are finite; a program needn't handle non-finite values.
Results may differ from a plain program's by a relative error of at most 0.0003.
Values sent between devices are 32-bit elements; how exact they have to be, the bound alone decides.
No kernel may reach another device: no remote copies, remote signals or barrier semaphores. Data moves between devices by JAX's collectives and lax.ppermute only.
A program may use at most 64 MiB of HBM per device.

v0:
```python
import jax
import jax.numpy as jnp
import numpy as np
from jax import lax
from jax.experimental import pallas as pl
from jax.experimental.pallas import tpu as pltpu
from jax.sharding import PartitionSpec as P

CELL_EDGE = 1.1
CUT_SQUARE = 1.0
SOFTEN = 0.09
ENERGY_UNIT = 0.1
EDGE_T = CUT_SQUARE + SOFTEN
K1 = EDGE_T**-0.5
K3 = EDGE_T**-3.0
K6 = EDGE_T**-6.0
OFFSETS = (
    (0, 0, 0),
    (0, 0, 1),
    (0, 1, 0),
    (0, 1, 1),
    (0, 1, -1),
) + tuple((1, oy, oz) for oy in (-1, 0, 1) for oz in (-1, 0, 1))
ROWS = 32


def shifted(block, axis, distance):
    devices = range(lax.axis_size(axis))
    route = [((i - distance) % len(devices), i) for i in devices]
    return lax.ppermute(block, axis, route)


def allowed(offset, at_low, at_high):
    if at_low:
        return offset >= 0
    if at_high:
        return offset < 0
    return True


def pair_kernel(counts_ref, feats_ref, table_ref, left_ref, forces_ref, fe, types, rows_a, fa, fb, eacc):
    ext_x, ext_y, ext_z = feats_ref.shape[:3]
    cells_x, cells_y, cells_z = ext_x - 1, ext_y - 1, ext_z - 1
    slots = feats_ref.shape[-1]
    row_id = lax.broadcasted_iota(jnp.int32, (8, slots), 0)
    eacc[...] = jnp.zeros_like(eacc)

    def place(ix, iy, iz):
        f = feats_ref[ix, iy, iz]
        shift = jnp.where(row_id == 0, ix, jnp.where(row_id == 1, iy, jnp.where(row_id == 2, iz, 0)))
        fe[ix, iy, iz] = f + shift.astype(jnp.float32) * CELL_EDGE
        types[ix, iy, iz] = f[4:5].astype(jnp.int32)
        fb[ix, iy, iz] = jnp.zeros(fb.shape[3:], jnp.float32)

    def place_plane(plane, _):
        ix = plane // ext_y
        iy = plane % ext_y
        for iz in range(ext_z):
            place(ix, iy, iz)
        return 0

    lax.fori_loop(0, ext_x * ext_y, place_plane, 0)

    lane_of = lax.broadcasted_iota(jnp.int32, (slots, slots), 1).astype(jnp.float32)
    f32, bf16 = jnp.float32, jnp.bfloat16

    def prepare(ix, iy, iz, slot):
        f = fe[ix, iy, iz]
        high = f.astype(bf16).astype(f32)
        mid = (f - high).astype(bf16).astype(f32)
        parts = jnp.concatenate([high, mid, f - high - mid], axis=0).T.astype(bf16)
        mine = jnp.dot(parts, left_ref[...], preferred_element_type=f32)
        hot = (mine[:, 4 * slots :] == lane_of).astype(f32).astype(bf16)
        looked = jnp.dot(jnp.concatenate([hot, hot], axis=1), table_ref[...], preferred_element_type=f32)
        for k in range(4):
            rows_a[slot, k] = mine[:, k * slots : (k + 1) * slots]
        for k in range(2):
            rows_a[slot, 4 + k] = looked[:, k * slots : (k + 1) * slots]

    def row_cell(ix, iy, iz, slot, offsets):
        count = counts_ref[ix, iy, iz]
        full = (count + (ROWS // 2 - 1)) // ROWS
        part = (count - full * ROWS + (ROWS - 1)) // ROWS

        def chunk(c, energy, rows):
            at = pl.multiple_of(c * ROWS, ROWS)
            here = pl.ds(at, rows)
            ax, ay, az, aq, a6, a12 = (rows_a[slot, k, here, :] for k in range(6))
            fx = fy = fz = None
            for ox, oy, oz in offsets:
                cell = (ix + ox, iy + oy, iz + oz)
                spread = lambda k: jnp.broadcast_to(fe[cell[0], cell[1], cell[2], k : k + 1, :], (rows, slots))
                dx = spread(0) - ax
                dy = spread(1) - ay
                dz = spread(2) - az
                qq = spread(3) * aq
                kind = jnp.broadcast_to(types[cell[0], cell[1], cell[2]], (rows, slots))
                c6, c12 = (
                    jnp.take_along_axis(t, kind, axis=1, mode="promise_in_bounds") for t in (a6, a12)
                )
                t = dx * dx + dy * dy + (dz * dz + SOFTEN)
                y = lax.rsqrt(t)
                v = y * y
                v3 = v * v * v
                p = qq * y
                h = c12 * v3
                m = h - c6
                gap = v3 - K3
                u = qq * (y - K1) + gap * m
                z = p + (6.0 * v3) * (m + c12 * gap)
                w = jnp.maximum(EDGE_T - t, 0.0)
                if (ox, oy, oz) == (0, 0, 0):
                    lane = lax.broadcasted_iota(jnp.int32, (rows, slots), 1)
                    row = lax.broadcasted_iota(jnp.int32, (rows, slots), 0) + at
                    w = jnp.where(lane > row, w, 0.0)
                s = w * ((w * v) * z + 4.0 * u)
                e = w * (w * u)
                for r in range(0, rows, 8):
                    energy = energy + e[r : r + 8]
                px, py, pz = s * dx, s * dy, s * dz
                for k, part in enumerate((px, py, pz)):
                    fold = part[0:8]
                    for r in range(8, rows, 8):
                        fold = fold + part[r : r + 8]
                    fb[cell[0], cell[1], cell[2], k] = fb[cell[0], cell[1], cell[2], k] + fold
                if fx is None:
                    fx, fy, fz = px, py, pz
                else:
                    fx, fy, fz = fx + px, fy + py, fz + pz
            for k, part in enumerate((fx, fy, fz)):
                fa[slot, k, here, :] = part
            return energy

        energy = lax.fori_loop(0, full, lambda c, e: chunk(c, e, ROWS), eacc[...])
        eacc[...] = lax.fori_loop(full, full + part, lambda c, e: chunk(c, e, ROWS // 2), energy)

    lane8 = lax.broadcasted_iota(jnp.int32, (slots, slots), 1)

    def finish(ix, iy, iz, slot):
        sums = [jnp.sum(fa[slot, k], axis=1, keepdims=True) for k in range(3)]
        packed = jnp.where(lane8 == 0, sums[0], jnp.where(lane8 == 1, sums[1], jnp.where(lane8 == 2, sums[2], 0.0)))
        forces_ref[ix, iy, iz] = -packed.T[:8]

    def row_line(ix, iy, low, high):
        fa[...] = jnp.zeros_like(fa)
        for iz in range(ext_z):
            prepare(ix, iy, iz, iz)

        def cells_at(iz, z_low, z_high):
            offsets = [
                o for o in OFFSETS if allowed(o[1], low, high) and allowed(o[2], z_low, z_high)
            ]
            row_cell(ix, iy, iz, iz, offsets)

        cells_at(0, True, False)

        def middle(iz, _):
            cells_at(iz, False, False)
            return 0

        lax.fori_loop(1, cells_z, middle, 0)
        cells_at(cells_z, False, True)
        for iz in range(ext_z):
            finish(ix, iy, iz, iz)

    def layer(ix, _):
        row_line(ix, 0, True, False)

        def middle(iy, _):
            row_line(ix, iy, False, False)
            return 0

        lax.fori_loop(1, cells_y, middle, 0)
        row_line(ix, cells_y, False, True)
        return 0

    lax.fori_loop(0, cells_x, layer, 0)

    energy_row = jnp.sum(eacc[...], axis=0, keepdims=True)

    def close(plane, _):
        ix = plane // ext_y
        iy = plane % ext_y
        for iz in range(ext_z):
            parts = [jnp.sum(fb[ix, iy, iz, k], axis=0, keepdims=True) for k in range(3)]
            total = jnp.concatenate(parts + [energy_row, jnp.zeros((4, slots), f32)], axis=0)
            held = jnp.where(ix < cells_x, forces_ref[ix, iy, iz], 0.0)
            forces_ref[ix, iy, iz] = held + total
        return 0

    lax.fori_loop(0, ext_x * ext_y, close, 0)


def pair_call(counts, feats, tables):
    ext = feats.shape[:3]
    slots = feats.shape[-1]
    f32 = jnp.float32
    left = np.zeros((24, 5 * slots), np.float32)
    for k in range(5):
        for n in range(3):
            left[8 * n + k, k * slots : (k + 1) * slots] = 1.0
    vmem = pl.BlockSpec(memory_space=pltpu.VMEM)
    return pl.pallas_call(
        pair_kernel,
        out_shape=jax.ShapeDtypeStruct(ext + (8, slots), f32),
        in_specs=[pl.BlockSpec(memory_space=pltpu.SMEM), vmem, vmem, vmem],
        out_specs=vmem,
        scratch_shapes=[
            pltpu.VMEM(ext + (8, slots), f32),
            pltpu.VMEM(ext + (1, slots), jnp.int32),
            pltpu.VMEM((ext[2], 6, slots, slots), f32),
            pltpu.VMEM((ext[2], 3, slots, slots), f32),
            pltpu.VMEM(ext + (3, 8, slots), f32),
            pltpu.VMEM((8, slots), f32),
        ],
        name="pair_forces",
    )(counts, feats, tables, jnp.asarray(left, jnp.bfloat16))


def make_tables(c6_table, c12_table, slots):
    c6 = (0.5 * ENERGY_UNIT) * (c6_table + c6_table.T)
    c12 = (0.5 * ENERGY_UNIT) * (c12_table + c12_table.T)
    more = slots - c6.shape[0]
    full = jnp.concatenate([jnp.pad(m, ((0, more), (0, more))) for m in (c6 - c12 * K3, c12)], axis=1)
    high = lax.reduce_precision(full, 8, 7)
    return jnp.concatenate([high, full - high], axis=0).astype(jnp.bfloat16)


def on_device(coords, charges, atom_types, counts, c6_table, c12_table):
    slots = coords.shape[-1]
    cells_x, cells_y, cells_z = coords.shape[:3]
    tables = make_tables(c6_table, c12_table, slots)
    occupied = jnp.arange(slots, dtype=jnp.int32) < counts[..., None]
    q = jnp.where(occupied, charges * ENERGY_UNIT**0.5, 0.0)
    kind = jnp.where(occupied, atom_types, slots - 1).astype(jnp.float32)
    held = jnp.broadcast_to(counts.astype(jnp.float32)[..., None], q.shape)
    rest = jnp.zeros(q.shape[:3] + (2, slots), jnp.float32)
    packed = jnp.concatenate(
        [coords, q[..., None, :], kind[..., None, :], held[..., None, :], rest], axis=3
    )
    extended = jnp.concatenate([packed, shifted(packed[:, :, :1], "gz", -1)], axis=2)
    side = shifted(extended[:, :1], "gy", -1)
    above = shifted(extended[:1], "gx", -1)
    corner = diagonal(extended[:1, :1])
    extended = jnp.concatenate(
        [jnp.concatenate([extended, side], axis=1), jnp.concatenate([above, corner], axis=1)], axis=0
    )
    row_counts = extended[:cells_x, :, :, 5, 0].astype(jnp.int32)
    forces = pair_call(row_counts, extended, tables)
    forces = give_back(forces, 2, "gz")
    forces = give_back(forces, 1, "gy")
    own = forces[0, 0, 0, 3]
    forces = give_back(forces, 0, "gx")
    return (forces[:, :, :, :3], jnp.sum(gathered(own, "gx", forces[0, 0, 0, 3])).reshape(1))


def diagonal(block):
    nx, ny = lax.axis_size("gx"), lax.axis_size("gy")
    route = [
        (((i + 1) % nx) * ny + (j + 1) % ny, i * ny + j) for i in range(nx) for j in range(ny)
    ]
    return lax.ppermute(block, ("gx", "gy"), route)


def gathered(own, axis, with_last):
    size = lax.axis_size(axis)
    if size == 1:
        return own
    if size > 4:
        return lax.psum(own, axis)
    for distance in range(2, size):
        with_last = with_last + shifted(own, axis, distance)
    return with_last


def give_back(forces, dim, axis):
    cells = forces.shape[dim] - 1
    kept = lax.slice_in_dim(forces, 0, cells, axis=dim)
    returned = shifted(lax.slice_in_dim(forces, cells, cells + 1, axis=dim), axis, 1)
    first = lax.slice_in_dim(kept, 0, 1, axis=dim) + returned
    if dim > 0 and lax.axis_size(axis) != 2:
        row = gathered(forces[0, 0, 0, 3], axis, first[0, 0, 0, 3])
        first = first.at[:, :, :, 3].set(row)
    return jnp.concatenate([first, lax.slice_in_dim(kept, 1, cells, axis=dim)], axis=dim)


def solution(mesh):
    return jax.shard_map(
        on_device,
        mesh=mesh,
        in_specs=(
            P(("groups", "gx"), "gy", "gz", None, None),
            P(("groups", "gx"), "gy", "gz", None),
            P(("groups", "gx"), "gy", "gz", None),
            P(("groups", "gx"), "gy", "gz"),
            P(),
            P(),
        ),
        out_specs=(P(("groups", "gx"), "gy", "gz", None, None), P("groups")),
        check_vma=False,
    )
```

profile of v0, /device:TPU:0, one launch (start us, length us, event | category | flops | bytes accessed | tf_op | source)
XLA Modules:
  0.0 91.4 jit_solution(3261851099315724650)
XLA Ops:
  0.6 0.7 convert_bitcast_fusion
  1.4 0.8 multiply_select_fusion
  2.2 0.8 select_convert_fusion
  3.0 0.1 broadcast_in_dim_broadcast_in_dim.2
  3.1 0.1 concatenate.28
  3.2 0.0 copy-start
  3.3 0.0 copy-start.1
  3.3 0.6 collective-permute-start
  3.8 0.2 copy-done
  4.0 0.1 copy.17
  4.1 0.1 copy.18
  4.2 0.5 collective-permute-done
  4.7 5.0 %collective-permute-start.2 = (f32[1,4,9,8,128]{4,3,2,1,0:T(8,128)S(1)}, f32[1,4,9,8,128]{4,3,2,1,0:T(8,128)S(1)}, u32[]{:S(2)}, u32[]{:S(2)}) collective-permute-start(f32[1,4,9,8,128]{4,3,2,1,0:T(8,128)S(1)} %pad_maximum_fusion), channel_id=1, source_target_pairs={{4,0},{8,4},{12,8},{0,12},{5,1},{9,5},{13,9},{1,13},{6,2},{10,6},{... | collective-permute-start | bytes 442376 | tf_op jit(solution)/shard_map/ppermute | solution.py:30
  9.7 1.4 %collective-permute-start.3 = (f32[1,1,9,8,128]{4,3,2,1,0:T(8,128)S(1)}, f32[1,1,9,8,128]{4,3,2,1,0:T(8,128)S(1)}, u32[]{:S(2)}, u32[]{:S(2)}) collective-permute-start(f32[1,1,9,8,128]{4,3,2,1,0:T(8,128)S(1)} %fusion.2), channel_id=1, source_target_pairs={{6,0},{4,2},{10,4},{8,6},{14,8},{12,10},{2,12},{0,14},{7,1},{5,3},... | collective-permute-start | bytes 110600 | tf_op jit(solution)/shard_map/ppermute | solution.py:262
  11.1 0.5 collective-permute-start.1
  11.6 0.7 pad_maximum_fusion.1.table_ref
  12.3 2.8 %collective-permute-done.1 = f32[1,1,9,8,128]{4,3,2,1,0:T(8,128)S(1)} collective-permute-done((f32[1,1,9,8,128]{4,3,2,1,0:T(8,128)S(1)}, f32[1,1,9,8,128]{4,3,2,1,0:T(8,128)S(1)}, u32[]{:S(2)}, u32[]{:S(2)}) %collective-permute-start.1) | collective-permute-done | bytes 36896 | tf_op jit(solution)/shard_map/ppermute | solution.py:30
  15.0 1.5 %fusion.6 = s32[5,9]{1,0:T(8,128)} fusion(f32[1,1,9,8,128]{4,3,2,1,0:T(8,128)S(1)} %collective-permute-done.1, f32[1,4,1,8,128]{4,3,2,1,0:T(8,128)S(1)} %collective-permute-done, f32[1,4,8,8,128]{4,3,2,1,0:T(8,128)S(1)} %concatenate.28), kind=kLoop, calls=%fused_computation.26 | loop fusion | flops 135 | bytes 184500 | tf_op jit(solution)/shard_map/convert_element_type | solution.py:248
  16.5 0.8 maximum_maximum_fusion.feats_ref
  17.3 58.0 %pair_forces.1 = f32[2,5,9,8,128]{4,3,2,1,0:T(8,128)} custom-call(s32[1,5,9]{2,1,0:T(8,128)} %bitcast.35, f32[2,5,9,8,128]{4,3,2,1,0:T(8,128)} %maximum_maximum_fusion.feats_ref, bf16[256,256]{1,0:T(8,128)(2,1)} %pad_maximum_fusion.1.table_ref, bf16[24,640]{1,0:T(8,128)(2,1)} %constant.16.clone.left_ref), custom_call_target="tpu_custom_call" | custom-call | tf_op jit(solution)/shard_map/pair_forces/pallas_call | solution.py:203
  75.3 0.8 slice.67
  76.0 1.0 %slice.68 = f32[2,5,7,8,128]{4,3,2,1,0:T(8,128)S(1)} slice(f32[2,5,9,8,128]{4,3,2,1,0:T(8,128)} %pair_forces.1), slice={[0:2], [0:5], [1:8], [0:8], [0:128]} | slice | bytes 573440 | tf_op jit(solution)/shard_map/slice | solution.py:284
  77.0 0.2 collective-permute-done.4
  77.3 0.8 slice_add_fusion.1
  78.1 0.8 collective-permute-start.5
  78.9 3.5 %collective-permute-done.5 = f32[2,1,8,8,128]{4,3,2,1,0:T(8,128)S(1)} collective-permute-done((f32[2,1,8,8,128]{4,3,2,1,0:T(8,128)S(1)}, f32[2,1,8,8,128]{4,3,2,1,0:T(8,128)S(1)}, u32[]{:S(2)}, u32[]{:S(2)}) %collective-permute-start.5) | collective-permute-done | bytes 65568 | tf_op jit(solution)/shard_map/ppermute | solution.py:30
  82.5 0.1 collective-permute-start.6
  82.5 3.8 %collective-permute-start.8 = (f32[128]{0:T(128)S(1)}, f32[128]{0:T(128)S(1)}, u32[]{:S(2)}, u32[]{:S(2)}) collective-permute-start(f32[128]{0:T(128)S(1)} %slice_bitcast_fusion), channel_id=1, source_target_pairs={{4,0},{8,4},{12,8},{0,12},{5,1},{9,5},{13,9},{1,13},{6,2},{10,6},{... | collective-permute-start | bytes 1544 | tf_op jit(solution)/shard_map/ppermute | solution.py:30
  86.3 2.9 %collective-permute-done.6 = f32[1,4,8,8,128]{4,3,2,1,0:T(8,128)S(1)} collective-permute-done((f32[1,4,8,8,128]{4,3,2,1,0:T(8,128)S(1)}, f32[1,4,8,8,128]{4,3,2,1,0:T(8,128)S(1)}, u32[]{:S(2)}, u32[]{:S(2)}) %collective-permute-start.6) | collective-permute-done | bytes 131104 | tf_op jit(solution)/shard_map/ppermute | solution.py:30
  89.3 0.6 copy.20
  90.0 0.9 collective-permute-done.7
  90.8 0.6 fusion.9
  (24 shorter events, 0.2 us)
Async XLA Ops:
  0.6 0.8 copy-start.3
  0.6 2.3 %copy-start.2 = (f32[1,4,8,3,128]{4,2,3,1,0:T(8,128)S(1)}, f32[1,4,8,3,128]{4,2,3,1,0:T(8,128)}, u32[]{:S(2)}) copy-start(f32[1,4,8,3,128]{4,2,3,1,0:T(8,128)} %param.7) | copy-start | bytes 147460
  3.2 0.8 copy-start
  3.3 0.8 copy-start.1
  3.3 1.4 %collective-permute-start = (f32[1,4,1,8,128]{4,3,2,1,0:T(8,128)S(1)}, f32[1,4,1,8,128]{4,3,2,1,0:T(8,128)S(1)}, u32[]{:S(2)}, u32[]{:S(2)}) collective-permute-start(f32[1,4,1,8,128]{4,3,2,1,0:T(8,128)S(1)} %slice.63), channel_id=1, source_target_pairs={{1,0},{0,1},{3,2},{2,3},{5,4},{4,5},{7,6},{6,7},{9,8},{8,9},{11,10... | collective-permute-start | bytes 49160 | tf_op jit(solution)/shard_map/ppermute | solution.py:30
  4.7 11.8 %collective-permute-start.2 = (f32[1,4,9,8,128]{4,3,2,1,0:T(8,128)S(1)}, f32[1,4,9,8,128]{4,3,2,1,0:T(8,128)S(1)}, u32[]{:S(2)}, u32[]{:S(2)}) collective-permute-start(f32[1,4,9,8,128]{4,3,2,1,0:T(8,128)S(1)} %pad_maximum_fusion), channel_id=1, source_target_pairs={{4,0},{8,4},{12,8},{0,12},{5,1},{9,5},{13,9},{1,13},{6,2},{10,6},{... | collective-permute-start | bytes 442376 | tf_op jit(solution)/shard_map/ppermute | solution.py:30
  9.7 6.8 %collective-permute-start.3 = (f32[1,1,9,8,128]{4,3,2,1,0:T(8,128)S(1)}, f32[1,1,9,8,128]{4,3,2,1,0:T(8,128)S(1)}, u32[]{:S(2)}, u32[]{:S(2)}) collective-permute-start(f32[1,1,9,8,128]{4,3,2,1,0:T(8,128)S(1)} %fusion.2), channel_id=1, source_target_pairs={{6,0},{4,2},{10,4},{8,6},{14,8},{12,10},{2,12},{0,14},{7,1},{5,3},... | collective-permute-start | bytes 110600 | tf_op jit(solution)/shard_map/ppermute | solution.py:262
  11.1 4.0 %collective-permute-start.1 = (f32[1,1,9,8,128]{4,3,2,1,0:T(8,128)S(1)}, f32[1,1,9,8,128]{4,3,2,1,0:T(8,128)S(1)}, u32[]{:S(2)}, u32[]{:S(2)}) collective-permute-start(f32[1,1,9,8,128]{4,3,2,1,0:T(8,128)S(1)} %fusion.2), channel_id=1, source_target_pairs={{2,0},{0,2},{3,1},{1,3},{6,4},{4,6},{7,5},{5,7},{10,8},{8,10},{11,... | collective-permute-start | bytes 110600 | tf_op jit(solution)/shard_map/ppermute | solution.py:30
  76.0 1.2 %collective-permute-start.4 = (f32[2,5,1,8,128]{4,3,2,1,0:T(8,128)S(1)}, f32[2,5,1,8,128]{4,3,2,1,0:T(8,128)S(1)}, u32[]{:S(2)}, u32[]{:S(2)}) collective-permute-start(f32[2,5,1,8,128]{4,3,2,1,0:T(8,128)S(1)} %slice.67), channel_id=1, source_target_pairs={{1,0},{0,1},{3,2},{2,3},{5,4},{4,5},{7,6},{6,7},{9,8},{8,9},{11,10... | collective-permute-start | bytes 122888 | tf_op jit(solution)/shard_map/ppermute | solution.py:30
  78.1 4.3 %collective-permute-start.5 = (f32[2,1,8,8,128]{4,3,2,1,0:T(8,128)S(1)}, f32[2,1,8,8,128]{4,3,2,1,0:T(8,128)S(1)}, u32[]{:S(2)}, u32[]{:S(2)}) collective-permute-start(f32[2,1,8,8,128]{4,3,2,1,0:T(8,128)S(1)} %pad_maximum_fusion.2), channel_id=1, source_target_pairs={{2,0},{0,2},{3,1},{1,3},{6,4},{4,6},{7,5},{5,7},{10,8},{8,10},{11,... | collective-permute-start | bytes 196616 | tf_op jit(solution)/shard_map/ppermute | solution.py:30
  82.5 6.8 %collective-permute-start.6 = (f32[1,4,8,8,128]{4,3,2,1,0:T(8,128)S(1)}, f32[1,4,8,8,128]{4,3,2,1,0:T(8,128)S(1)}, u32[]{:S(2)}, u32[]{:S(2)}) collective-permute-start(f32[1,4,8,8,128]{4,3,2,1,0:T(8,128)S(1)} %slice.70), channel_id=1, source_target_pairs={{12,0},{0,4},{4,8},{8,12},{13,1},{1,5},{5,9},{9,13},{14,2},{2,6},{... | collective-permute-start | bytes 393224 | tf_op jit(solution)/shard_map/ppermute | solution.py:30
  82.5 7.4 %collective-permute-start.8 = (f32[128]{0:T(128)S(1)}, f32[128]{0:T(128)S(1)}, u32[]{:S(2)}, u32[]{:S(2)}) collective-permute-start(f32[128]{0:T(128)S(1)} %slice_bitcast_fusion), channel_id=1, source_target_pairs={{4,0},{8,4},{12,8},{0,12},{5,1},{9,5},{13,9},{1,13},{6,2},{10,6},{... | collective-permute-start | bytes 1544 | tf_op jit(solution)/shard_map/ppermute | solution.py:30
  86.3 4.5 %collective-permute-start.7 = (f32[128]{0:T(128)S(1)}, f32[128]{0:T(128)S(1)}, u32[]{:S(2)}, u32[]{:S(2)}) collective-permute-start(f32[128]{0:T(128)S(1)} %slice_bitcast_fusion), channel_id=1, source_target_pairs={{8,0},{12,4},{0,8},{4,12},{9,1},{13,5},{1,9},{5,13},{10,2},{14,6},... | collective-permute-start | bytes 1544 | tf_op jit(solution)/shard_map/ppermute | solution.py:30
where the time goes:
time: 91.4 us
  Pallas kernels  58 us (63%)
  starting transfers between devices  12.1 us (13%)
  waiting for transfers between devices  10.8 us (12%)
  other arithmetic  6.76 us (7%)
  local copies, waits for them, and re-layouts  2.99 us (3%)
    pallas_call x1, Pallas kernels, pair_call(): pl.pallas_call(pair_kernel, out_shape=jax.ShapeDtypeStruct(ext + (8, slot...  58 us
    ppermute x8, waiting for transfers between devices, shifted(): return lax.ppermute(block, axis, route)  10.8 us
    ppermute x8, starting transfers between devices, shifted(): return lax.ppermute(block, axis, route)  10.8 us
  transfers between devices with their start and end apart: 9, of which 6 were waited for; matrix products, arithmetic and copies ran while one was open for 4% of the time, Pallas kernels for 0%

commit v1 on v0

v1 whole, which is shorter than its diff:
```python
import jax
import jax.numpy as jnp
import numpy as np
from jax import lax
from jax.experimental import pallas as pl
from jax.experimental.pallas import tpu as pltpu
from jax.sharding import PartitionSpec as P

CELL_EDGE = 1.1
CUT_SQUARE = 1.0
SOFTEN = 0.09
ENERGY_UNIT = 0.1
EDGE_T = CUT_SQUARE + SOFTEN
K1 = EDGE_T**-0.5
K3 = EDGE_T**-3.0
K6 = EDGE_T**-6.0
OFFSETS = (
    (0, 0, 0),
    (0, 0, 1),
    (0, 1, 0),
    (0, 1, 1),
    (0, 1, -1),
) + tuple((1, oy, oz) for oy in (-1, 0, 1) for oz in (-1, 0, 1))
ROWS = 32
AXES = ("gx", "gy", "gz")


def moved(block, dx, dy, dz):
    nx, ny, nz = (lax.axis_size(a) for a in AXES)
    flat = lambda i, j, k: ((i % nx) * ny + j % ny) * nz + k % nz
    cells = [(i, j, k) for i in range(nx) for j in range(ny) for k in range(nz)]
    route = [(flat(i - dx, j - dy, k - dz), flat(i, j, k)) for i, j, k in cells]
    return lax.ppermute(block, AXES, route)


def pack_kernel(counts_ref, coords_ref, charges_ref, types_ref, packed_ref, faces_ref):
    cells_x, cells_y, _, cells_z, slots = coords_ref.shape
    lane = lax.broadcasted_iota(jnp.int32, (1, slots), 1)
    for ix in range(cells_x):
        for iy in range(cells_y):
            for iz in range(cells_z):
                here = lane < counts_ref[ix, iy, iz]
                q = jnp.where(here, charges_ref[ix, iy, iz : iz + 1] * ENERGY_UNIT**0.5, 0.0)
                kind = jnp.where(here, types_ref[ix, iy, iz : iz + 1], slots - 1).astype(jnp.float32)
                place = [coords_ref[ix, iy, k, iz : iz + 1] for k in range(3)]
                cell = jnp.concatenate(place + [q, kind, jnp.zeros((3, slots), jnp.float32)], axis=0)
                packed_ref[ix, iy, iz] = cell
                for b, at in enumerate((0, cells_z - 1)):
                    if iz == at:
                        faces_ref[ix, iy, b] = cell


def whole_call(kernel, name, outs, operands, smem=0):
    vmem = pl.BlockSpec(memory_space=pltpu.VMEM)
    return pl.pallas_call(
        kernel,
        out_shape=tuple(jax.ShapeDtypeStruct(o, jnp.float32) for o in outs),
        in_specs=[pl.BlockSpec(memory_space=pltpu.SMEM)] * smem + [vmem] * (len(operands) - smem),
        out_specs=(vmem,) * len(outs),
        name=name,
    )(*operands)


def row_kernel(packed_ref, c6_ref, c12_ref, left_ref, rows_ref, table_ref):
    cells_z, _, slots = packed_ref.shape[2:]
    f32, bf16 = jnp.float32, jnp.bfloat16
    row_id = lax.broadcasted_iota(jnp.int32, (8, slots), 0)
    lane_of = lax.broadcasted_iota(jnp.int32, (slots, slots), 1).astype(f32)
    ix, iy = pl.program_id(0), pl.program_id(1) + 1

    @pl.when((pl.program_id(0) == 0) & (pl.program_id(1) == 0))
    def _():
        kinds = c6_ref.shape[0]
        table_ref[...] = jnp.zeros_like(table_ref)
        c6, c12 = ((0.5 * ENERGY_UNIT) * (c[...] + c[...].T) for c in (c6_ref, c12_ref))
        for k, table in enumerate((c6 - c12 * K3, c12)):
            high = table.astype(bf16)
            at = slice(k * slots, k * slots + kinds)
            table_ref[0:kinds, at] = high
            table_ref[slots : slots + kinds, at] = (table - high.astype(f32)).astype(bf16)

    for iz in range(cells_z):
        at = jnp.where(row_id == 0, ix, jnp.where(row_id == 1, iy, jnp.where(row_id == 2, iz + 1, 0)))
        f = packed_ref[0, 0, iz] + at.astype(f32) * CELL_EDGE
        high = f.astype(bf16).astype(f32)
        mid = (f - high).astype(bf16).astype(f32)
        parts = jnp.concatenate([high, mid, f - high - mid], axis=0).T.astype(bf16)
        mine = jnp.dot(parts, left_ref[...], preferred_element_type=f32)
        hot = (mine[:, 4 * slots :] == lane_of).astype(f32).astype(bf16)
        looked = jnp.dot(jnp.concatenate([hot, hot], axis=1), table_ref[...], preferred_element_type=f32)
        for k in range(4):
            rows_ref[0, iz, k] = mine[:, k * slots : (k + 1) * slots]
        for k in range(2):
            rows_ref[0, iz, 4 + k] = looked[:, k * slots : (k + 1) * slots]


def row_call(packed, c6_table, c12_table):
    cells_x, cells_y, cells_z, _, slots = packed.shape
    left = np.zeros((24, 5 * slots), np.float32)
    for k in range(5):
        for n in range(3):
            left[8 * n + k, k * slots : (k + 1) * slots] = 1.0
    left = jnp.asarray(left, jnp.bfloat16)
    atoms = cells_x * cells_y * cells_z * slots
    return pl.pallas_call(
        row_kernel,
        grid=(cells_x, cells_y),
        out_shape=jax.ShapeDtypeStruct((cells_x * cells_y, cells_z, 6, slots, slots), jnp.float32),
        in_specs=[
            pl.BlockSpec((1, 1, cells_z, 8, slots), lambda i, j: (i, j, 0, 0, 0)),
            pl.BlockSpec(c6_table.shape, lambda i, j: (0, 0)),
            pl.BlockSpec(c12_table.shape, lambda i, j: (0, 0)),
            pl.BlockSpec(left.shape, lambda i, j: (0, 0)),
        ],
        out_specs=pl.BlockSpec((1, cells_z, 6, slots, slots), lambda i, j: (i * cells_y + j, 0, 0, 0, 0)),
        scratch_shapes=[pltpu.VMEM((2 * slots, 2 * slots), jnp.bfloat16)],
        cost_estimate=pl.CostEstimate(
            flops=2 * atoms * slots * 376, transcendentals=0, bytes_accessed=atoms * slots * 24
        ),
        name="row_operands",
    )(packed, c6_table, c12_table, left)


def pair_kernel(
    counts_ref, packed_ref, pz_ref, py_ref, px_ref, pc_ref, rows_ref,
    own_ref, oz_ref, oy_ref, ozy_ref, ox_ref, fa,
    fe, types, fb, eacc,
):
    cells_x, cells_y, cells_z, _, slots = own_ref.shape
    ext_y, ext_z = cells_y + 2, cells_z + 2
    f32, bf16 = jnp.float32, jnp.bfloat16
    row_id = lax.broadcasted_iota(jnp.int32, (8, slots), 0)
    line = pl.program_id(0)

    @pl.when(line == 0)
    def _():
        eacc[...] = jnp.zeros_like(eacc)

        def place(f, ix, iy, iz):
            at = jnp.where(row_id == 0, ix, jnp.where(row_id == 1, iy, jnp.where(row_id == 2, iz, 0)))
            fe[ix, iy, iz] = f + at.astype(f32) * CELL_EDGE
            types[ix, iy, iz] = f[4:5].astype(jnp.int32)
            fb[ix, iy, iz] = jnp.zeros(fb.shape[3:], f32)

        def place_line(iy, _):
            for ix in range(cells_x):
                for iz in range(cells_z):
                    place(packed_ref[ix, iy, iz], ix, iy + 1, iz + 1)
                place(pz_ref[ix, iy, 0], ix, iy + 1, cells_z + 1)
                place(pz_ref[ix, iy, 1], ix, iy + 1, 0)
            for iz in range(ext_z):
                place(px_ref[0, iy, iz], cells_x, iy + 1, iz)
            return 0

        lax.fori_loop(0, cells_y, place_line, 0)
        for iz in range(ext_z):
            for ix in range(cells_x):
                place(py_ref[ix, 0, iz], ix, cells_y + 1, iz)
                fb[ix, 0, iz] = jnp.zeros(fb.shape[3:], f32)
            place(pc_ref[0, 0, iz], cells_x, cells_y + 1, iz)
            place(pc_ref[0, 1, iz], cells_x, 0, iz)

    def row_cell(ix, iy, iz, slot, offsets):
        count = counts_ref[ix, iy, iz]
        quarters = (count + (ROWS // 4 - 1)) // (ROWS // 4)
        full = quarters // 4
        half = (quarters // 2) % 2
        rest = quarters % 2

        def chunk(at, energy, rows):
            at = pl.multiple_of(at, rows)
            here = pl.ds(at, rows)
            ax, ay, az, aq, a6, a12 = (rows_ref[0, slot, k, here, :] for k in range(6))
            fx = fy = fz = None
            for ox, oy, oz in offsets:
                cell = (ix + ox, iy + 1 + oy, iz + 1 + oz)
                spread = lambda k: jnp.broadcast_to(fe[cell[0], cell[1], cell[2], k : k + 1, :], (rows, slots))
                dx = spread(0) - ax
                dy = spread(1) - ay
                dz = spread(2) - az
                qq = spread(3) * aq
                kind = jnp.broadcast_to(types[cell[0], cell[1], cell[2]], (rows, slots))
                c6, c12 = (
                    jnp.take_along_axis(t, kind, axis=1, mode="promise_in_bounds") for t in (a6, a12)
                )
                t = dx * dx + dy * dy + (dz * dz + SOFTEN)
                y = lax.rsqrt(t)
                v = y * y
                v3 = v * v * v
                p = qq * y
                h = c12 * v3
                m = h - c6
                gap = v3 - K3
                u = qq * (y - K1) + gap * m
                z = p + (6.0 * v3) * (m + c12 * gap)
                w = jnp.maximum(EDGE_T - t, 0.0)
                if (ox, oy, oz) == (0, 0, 0):
                    lane = lax.broadcasted_iota(jnp.int32, (rows, slots), 1)
                    row = lax.broadcasted_iota(jnp.int32, (rows, slots), 0) + at
                    w = jnp.where(lane > row, w, 0.0)
                s = w * ((w * v) * z + 4.0 * u)
                e = w * (w * u)
                for r in range(0, rows, 8):
                    energy = energy + e[r : r + 8]
                px, py, pz = s * dx, s * dy, s * dz
                for k, part in enumerate((px, py, pz)):
                    fold = part[0:8]
                    for r in range(8, rows, 8):
                        fold = fold + part[r : r + 8]
                    fb[cell[0], cell[1], cell[2], k] = fb[cell[0], cell[1], cell[2], k] + fold
                if fx is None:
                    fx, fy, fz = px, py, pz
                else:
                    fx, fy, fz = fx + px, fy + py, fz + pz
            for k, part in enumerate((fx, fy, fz)):
                fa[0, slot, k, here, :] = part
            return energy

        energy = lax.fori_loop(0, full, lambda c, e: chunk(c * ROWS, e, ROWS), eacc[...])
        energy = lax.fori_loop(0, half, lambda c, e: chunk(full * ROWS, e, ROWS // 2), energy)
        last = full * ROWS + half * (ROWS // 2)
        eacc[...] = lax.fori_loop(0, rest, lambda c, e: chunk(last, e, ROWS // 4), energy)

    ix = line // cells_y
    iy = line % cells_y
    fa[...] = jnp.zeros_like(fa)

    def inner(iz, _):
        row_cell(ix, iy, iz, iz, OFFSETS)
        return 0

    lax.fori_loop(0, cells_z, inner, 0)
    @pl.when(line == pl.num_programs(0) - 1)
    def _():
        energy = jnp.sum(eacc[...], axis=0, keepdims=True)

        def total_of(ix, iy, iz):
            parts = [jnp.sum(fb[ix, iy, iz, k], axis=0, keepdims=True) for k in range(3)]
            return jnp.concatenate(parts + [energy, jnp.zeros((4, slots), f32)], axis=0)

        def close_line(iy, _):
            for ix in range(cells_x + 1):
                for iz in range(cells_z):
                    if ix < cells_x:
                        own_ref[ix, iy, iz] = total_of(ix, iy + 1, iz + 1)
                    else:
                        ox_ref[0, iy, iz] = total_of(ix, iy + 1, iz + 1)
                for b, at_z in enumerate((0, cells_z + 1)):
                    oz_ref[ix, iy, b] = total_of(ix, iy + 1, at_z)
            return 0

        lax.fori_loop(0, cells_y, close_line, 0)
        for ix in range(cells_x + 1):
            for a, at_y in enumerate((0, cells_y + 1)):
                for iz in range(cells_z):
                    oy_ref[ix, a, iz] = total_of(ix, at_y, iz + 1)
                for b, at_z in enumerate((0, cells_z + 1)):
                    ozy_ref[ix, a, b] = total_of(ix, at_y, at_z)


def pair_call(counts, pieces, rows):
    cells_x, cells_y, cells_z = counts.shape
    slots = rows.shape[-1]
    f32 = jnp.float32
    fixed = lambda shape: pl.BlockSpec(shape, lambda i: (0,) * len(shape))
    outs = [
        dims + (8, slots)
        for dims in (
            (cells_x, cells_y, cells_z),
            (cells_x + 1, cells_y, 2),
            (cells_x + 1, 2, cells_z),
            (cells_x + 1, 2, 2),
            (1, cells_y, cells_z),
        )
    ]
    sums = (cells_x * cells_y, cells_z, 3, slots, slots)
    by_line = lambda shape: pl.BlockSpec((1,) + shape[1:], lambda i: (i, 0, 0, 0, 0))
    grown = (cells_x + 1, cells_y + 2, cells_z + 2)
    return pl.pallas_call(
        pair_kernel,
        grid=(cells_x * cells_y,),
        out_shape=tuple(jax.ShapeDtypeStruct(o, f32) for o in outs + [sums]),
        in_specs=[pl.BlockSpec(memory_space=pltpu.SMEM)]
        + [fixed(piece.shape) for piece in pieces]
        + [by_line(rows.shape)],
        out_specs=tuple(fixed(o) for o in outs) + (by_line(sums),),
        scratch_shapes=[
            pltpu.VMEM(grown + (8, slots), f32),
            pltpu.VMEM(grown + (1, slots), jnp.int32),
            pltpu.VMEM(grown + (3, 8, slots), f32),
            pltpu.VMEM((8, slots), f32),
        ],
        name="pair_forces",
    )(counts, *pieces, rows)


def own_kernel(sums_ref, own_ref, ends_ref, out_ref):
    f32, bf16 = jnp.float32, jnp.bfloat16
    for iz in range(sums_ref.shape[1]):
        halves = []
        for k in range(3):
            whole = sums_ref[0, iz, k]
            high = whole.astype(bf16)
            halves += [high, (whole - high.astype(f32)).astype(bf16)]
        total = jnp.dot(jnp.concatenate(halves, axis=1), ends_ref[...], preferred_element_type=f32)
        out_ref[0, 0, iz] = own_ref[0, 0, iz] - total.T[:8]


def own_call(sums, own):
    cells_x, cells_y, cells_z, _, slots = own.shape
    ends = np.zeros((6 * slots, slots), np.float32)
    for k in range(3):
        ends[2 * k * slots : 2 * (k + 1) * slots, k] = 1.0
    ends = jnp.asarray(ends, jnp.bfloat16)
    block = pl.BlockSpec((1, 1, cells_z, 8, slots), lambda i, j: (i, j, 0, 0, 0))
    return pl.pallas_call(
        own_kernel,
        grid=(cells_x, cells_y),
        out_shape=jax.ShapeDtypeStruct(own.shape, jnp.float32),
        in_specs=[
            pl.BlockSpec((1,) + sums.shape[1:], lambda i, j: (i * cells_y + j, 0, 0, 0, 0)),
            block,
            pl.BlockSpec(ends.shape, lambda i, j: (0, 0)),
        ],
        out_specs=block,
        cost_estimate=pl.CostEstimate(
            flops=8 * sums.size, transcendentals=0, bytes_accessed=4 * sums.size
        ),
        name="own_rows",
    )(sums, own, ends)


def final_kernel(own_ref, rz_ref, ry_ref, rzy_ref, rx_ref, *refs):
    *terms, forces_ref, energy_ref = refs
    cells_x, cells_y, cells_z, _, slots = own_ref.shape
    for ix in range(cells_x):
        for iy in range(cells_y):
            sides_y = [m for m, at in enumerate((cells_y - 1, 0)) if iy == at]
            for iz in range(cells_z):
                sides_z = [n for n, at in enumerate((cells_z - 1, 0)) if iz == at]
                f = own_ref[ix, iy, iz]
                for n in sides_z:
                    f = f + rz_ref[ix, iy, n]
                for m in sides_y:
                    f = f + ry_ref[ix, m, iz]
                    for n in sides_z:
                        f = f + rzy_ref[ix, m, n]
                if ix == 0:
                    f = f + rx_ref[0, iy, iz]
                if ix == 0 and iy == 0 and iz == 0:
                    energy = f[3:4]
                for k in range(3):
                    forces_ref[ix, iy, k, iz : iz + 1] = f[k : k + 1]
    for term in terms:
        energy = energy + term[...]
    energy_ref[...] = jnp.broadcast_to(jnp.sum(energy, axis=1, keepdims=True), (1, slots))


def both_ways(block, dim, step, size):
    if size == 2:
        return moved(block, *step)
    down = moved(lax.slice_in_dim(block, 0, 1, axis=dim), *(-d for d in step))
    up = moved(lax.slice_in_dim(block, 1, 2, axis=dim), *step)
    return jnp.concatenate([down, up], axis=dim)


def to_sides(z, y, zy, ny, nz):
    if ny == 2 and nz == 2:
        corners = moved(zy, 0, 1, 1)
    else:
        corners = jnp.concatenate(
            [
                jnp.concatenate(
                    [moved(zy[:, a : a + 1, b : b + 1], 0, 2 * a - 1, 2 * b - 1) for b in range(2)], axis=2
                )
                for a in range(2)
            ],
            axis=1,
        )
    return both_ways(z, 2, (0, 0, 1), nz), both_ways(y, 1, (0, 1, 0), ny), corners


def spread(block, dim, size):
    zeros = jnp.zeros(block.shape[:dim] + (size - 2,) + block.shape[dim + 1 :], block.dtype)
    down, up = (lax.slice_in_dim(block, m, m + 1, axis=dim) for m in range(2))
    return jnp.concatenate([up, zeros, down], axis=dim)


def on_device(coords, charges, atom_types, counts, c6_table, c12_table):
    slots = coords.shape[-1]
    cells_x, cells_y, cells_z = coords.shape[:3]
    nx, ny, nz = (lax.axis_size(a) for a in AXES)
    tail = (8, slots)
    packed, faces = whole_call(
        pack_kernel,
        "pack_cells",
        [(cells_x, cells_y, cells_z) + tail, (cells_x, cells_y, 2) + tail],
        (counts, jnp.swapaxes(coords, 2, 3), charges, atom_types),
        smem=1,
    )
    pz = both_ways(faces, 2, (0, 0, 1), nz)
    lines = jnp.concatenate([pz[:, :, 1:], packed, pz[:, :, :1]], axis=2)
    ends = jnp.concatenate([lines[:1, :1], lines[:1, cells_y - 1 :]], axis=1)
    px = moved(lines[:1], -1, 0, 0)
    py = moved(lines[:, :1], 0, -1, 0)
    if ny == 2:
        pc = moved(ends, -1, -1, 0)
    else:
        pc = jnp.concatenate([moved(ends[:, :1], -1, -1, 0), moved(ends[:, 1:], -1, 1, 0)], axis=1)
    rows = row_call(packed, c6_table, c12_table)
    own, oz, oy, ozy, ox, sums = pair_call(counts, (packed, pz, py, px, pc), rows)
    rz, ry, rzy = to_sides(oz, oy, ozy, ny, nz)
    own, rz = lax.optimization_barrier((own_call(sums, own), rz))
    ox = (
        ox
        + spread(rz[cells_x:], 2, cells_z)
        + spread(ry[cells_x:], 1, cells_y)
        + spread(spread(rzy[cells_x:], 2, cells_z), 1, cells_y)
    )
    rx = moved(ox, 1, 0, 0)
    if nz == 2 and ny == 2 and 2 <= nx <= 4:
        summed = ox[0, 0, 0, 3:4]
        terms = [moved(summed, i, 0, 0) for i in range(2, nx)]
    else:
        terms = [lax.psum(own[0, 0, 0, 3:4], AXES)]
        rz, ry, rzy, rx = (r.at[..., 3, :].set(0.0) for r in (rz, ry, rzy, rx))
        own = own.at[..., 3, :].set(0.0)
    forces, energy = whole_call(
        final_kernel,
        "join_forces",
        [(cells_x, cells_y, 3, cells_z, slots), (1, slots)],
        (own, rz, ry, rzy, rx, *terms),
    )
    return (jnp.swapaxes(forces, 2, 3), energy[0, :1])


def solution(mesh):
    return jax.shard_map(
        on_device,
        mesh=mesh,
        in_specs=(
            P(("groups", "gx"), "gy", "gz", None, None),
            P(("groups", "gx"), "gy", "gz", None),
            P(("groups", "gx"), "gy", "gz", None),
            P(("groups", "gx"), "gy", "gz"),
            P(),
            P(),
        ),
        out_specs=(P(("groups", "gx"), "gy", "gz", None, None), P("groups")),
        check_vma=False,
    )
```

time: 91.4 us -> 85.9 us (0.940); the launches traced: 91.4 us -> 84.3 us
  waiting for transfers between devices: 10.8 us -> 4.04 us
  other arithmetic: 6.76 us -> 2.06 us
  Pallas kernels: 58 us -> 60.7 us
  starting transfers between devices: 12.1 us -> 14.6 us
    ppermute x9 -> x10, waiting for transfers between devices: 10.8 us -> 4.04 us  [moved(): return lax.ppermute(block, AXES, route)]
    convert_element_type x3 -> x0, other arithmetic: 3.04 us -> none  [the longest x1 1.51 us: on_device(): row_counts = extended[:cells_x, :, :, 5, 0].astype(jnp.int32)]
    pallas_call x1 -> x5, Pallas kernels: 58 us -> 60.7 us  [the longest x1 43.5 us: pair_call(): pl.pallas_call(pair_kernel, grid=(cells_x * cells_y,), out_shape=tuple((j...]
    ppermute x9 -> x10, starting transfers between devices: 12.1 us -> 14.6 us  [moved(): return lax.ppermute(block, AXES, route)]
    slice x5 -> x6, local copies, waits for them, and re-layouts: 1.79 us -> 0.03 us  [the longest x4 0.02 us: spread(): down, up = (lax.slice_in_dim(block, m, m + 1, axis=dim) for m in range(2))]
    unnamed x12 -> x20, local copies, waits for them, and re-layouts: 0.97 us -> 1.92 us
  transfers between devices with their start and end apart: 9 -> 10, of which waited for: 6 -> 4; matrix products, arithmetic and copies ran while one was open for 4% -> 0% of each run, Pallas kernels for 0% -> 16%
where the time goes in v1:
time: 85.9 us; the launch traced here: 84.3 us
  Pallas kernels  60.7 us (71%)
  starting transfers between devices  14.6 us (17%)
  waiting for transfers between devices  4.04 us (5%)
  local copies, waits for them, and re-layouts  2.11 us (2%)
  other arithmetic  2.06 us (2%)
    pallas_call x1, Pallas kernels, pair_call(): pl.pallas_call(pair_kernel, grid=(cells_x * cells_y,), out_shape=tuple((j...  43.5 us
    ppermute x10, starting transfers between devices, moved(): return lax.ppermute(block, AXES, route)  14.6 us
    pallas_call x1, Pallas kernels, row_call(): pl.pallas_call(row_kernel, grid=(cells_x, cells_y), out_shape=jax.ShapeDt...  8.49 us
    pallas_call x1, Pallas kernels, own_call(): pl.pallas_call(own_kernel, grid=(cells_x, cells_y), out_shape=jax.ShapeDt...  5.38 us
    ppermute x10, waiting for transfers between devices, moved(): return lax.ppermute(block, AXES, route)  4.04 us
    pallas_call x2, Pallas kernels, whole_call(): pl.pallas_call(kernel, out_shape=tuple((jax.ShapeDtypeStruct(o, jnp.float...  3.31 us
    unnamed x20, local copies, waits for them, and re-layouts  1.92 us
  transfers between devices with their start and end apart: 10, of which 4 were waited for; matrix products, arithmetic and copies ran while one was open for 0% of the time, Pallas kernels for 16%

profile of v1, /device:TPU:0, one launch (start us, length us, event | category | flops | bytes accessed | tf_op | source)
XLA Modules:
  0.0 84.3 jit_solution(16965293754254362629)
XLA Ops:
  0.6 1.6 %pack_cells.1 = (f32[1,4,8,8,128]{4,3,2,1,0:T(8,128)}, f32[1,4,2,8,128]{4,3,2,1,0:T(8,128)}) custom-call(s32[1,4,8]{2,1,0:T(4,128)} %counts_ref.3, f32[1,4,3,8,128]{4,3,2,1,0:T(8,128)} %bitcast.6, f32[1,4,8,128]{3,2,1,0:T(8,128)} %charges_ref.1, s32[1,4,8,128]{3,2,1,0:T(8,128)} %types_ref.1), custom_call_target="tpu_custom_call" | custom-call | tf_op jit(solution)/shard_map/pack_cells/pallas_call | solution.py:55
  2.2 0.5 collective-permute-start
  2.7 1.1 %collective-permute-done.pz_ref = f32[1,4,2,8,128]{4,3,2,1,0:T(8,128)S(1)} collective-permute-done((f32[1,4,2,8,128]{4,3,2,1,0:T(8,128)}, f32[1,4,2,8,128]{4,3,2,1,0:T(8,128)S(1)}, u32[]{:S(2)}, u32[]{:S(2)}) %collective-permute-start) | collective-permute-done | bytes 32800 | tf_op jit(solution)/shard_map/ppermute | solution.py:33
  3.8 0.9 %pad_maximum_fusion = f32[1,4,10,8,128]{4,3,2,1,0:T(8,128)S(1)} fusion(f32[1,4,1,8,128]{4,3,2,1,0:T(8,128)S(1)} %get-tuple-element.37, f32[1,4,8,8,128]{4,3,2,1,0:T(8,128)} %get-tuple-element.14.packed_ref, f32[1,4,1,8,128]{4,3,2,1,0:T(8,128)S(1)} %get-tuple-element.36), kind=kLoop, calls=%fused_computation | loop fusion | flops 81920 | bytes 327680 | tf_op jit(solution)/shard_map/concatenate | solution.py:402
  4.7 5.0 %collective-permute-start.2 = (f32[1,4,10,8,128]{4,3,2,1,0:T(8,128)S(1)}, f32[1,4,10,8,128]{4,3,2,1,0:T(8,128)S(1)}, u32[]{:S(2)}, u32[]{:S(2)}) collective-permute-start(f32[1,4,10,8,128]{4,3,2,1,0:T(8,128)S(1)} %pad_maximum_fusion), channel_id=1, source_target_pairs={{4,0},{5,1},{6,2},{7,3},{8,4},{9,5},{10,6},{11,7},{12,8},{13,9},{1... | collective-permute-start | bytes 491528 | tf_op jit(solution)/shard_map/ppermute | solution.py:33
  9.7 1.4 %collective-permute-start.3 = (f32[1,2,10,8,128]{4,3,2,1,0:T(8,128)S(1)}, f32[1,2,10,8,128]{4,3,2,1,0:T(8,128)S(1)}, u32[]{:S(2)}, u32[]{:S(2)}) collective-permute-start(f32[1,2,10,8,128]{4,3,2,1,0:T(8,128)S(1)} %pad_maximum_fusion.1), channel_id=1, source_target_pairs={{6,0},{7,1},{4,2},{5,3},{10,4},{11,5},{8,6},{9,7},{14,8},{15,9},{1... | collective-permute-start | bytes 245768 | tf_op jit(solution)/shard_map/ppermute | solution.py:33
  11.1 0.5 collective-permute-start.1
  11.6 8.5 %row_operands.1.rows_ref = f32[4,8,6,128,128]{4,3,2,1,0:T(8,128)} custom-call(f32[1,4,8,8,128]{4,3,2,1,0:T(8,128)} %get-tuple-element.14.packed_ref, f32[64,64]{1,0:T(8,128)} %c6_ref.1, f32[64,64]{1,0:T(8,128)} %c12_ref.1, bf16[24,640]{1,0:T(8,128)(2,1)} %constant.4.clone.left_ref), custom_call_target="tpu_custom_call" | custom-call | flops 394264576 | bytes 12582912 | tf_op jit(solution)/shard_map/row_operands/pallas_call | solution.py:105
  20.1 0.0 collective-permute-done.1.py_ref
  20.1 0.0 collective-permute-done.3.pc_ref
  20.1 0.0 collective-permute-done.2.px_ref
  20.2 0.6 copy-done.7
  20.7 0.0 copy-done.5
  20.8 0.7 copy-done.1
  21.4 43.5 %pair_forces.1 = (f32[1,4,8,8,128]{4,3,2,1,0:T(8,128)}, f32[2,4,2,8,128]{4,3,2,1,0:T(8,128)}, f32[2,2,8,8,128]{4,3,2,1,0:T(8,128)}, f32[2,2,2,8,128]{4,3,2,1,0:T...) custom-call(s32[1,4,8]{2,1,0:T(4,128)} %counts_ref.3, ...), custom_call_target="tpu_custom_call" | custom-call | tf_op jit(solution)/shard_map/pair_forces/pallas_call | solution.py:279
  64.9 2.4 %collective-permute-start.6 = (f32[2,2,2,8,128]{4,3,2,1,0:T(8,128)}, f32[2,2,2,8,128]{4,3,2,1,0:T(8,128)S(1)}, u32[]{:S(2)}, u32[]{:S(2)}) collective-permute-start(f32[2,2,2,8,128]{4,3,2,1,0:T(8,128)} %get-tuple-element.22), channel_id=1, source_target_pairs={{3,0},{2,1},{1,2},{0,3},{7,4},{6,5},{5,6},{4,7},{11,8},{10,9},{9,1... | collective-permute-start | bytes 98312 | tf_op jit(solution)/shard_map/ppermute | solution.py:33
  67.3 0.1 pad.10.clone
  67.4 0.1 pad.7.clone
  67.5 0.0 collective-permute-start.4
  67.5 0.4 collective-permute-start.5
  67.9 5.4 %own_rows.1.own_ref = f32[1,4,8,8,128]{4,3,2,1,0:T(8,128)} custom-call(f32[4,8,3,128,128]{4,3,2,1,0:T(8,128)} %get-tuple-element.16.sums_ref, f32[1,4,8,8,128]{4,3,2,1,0:T(8,128)} %get-tuple-element.17.own_ref, bf16[768,128]{1,0:T(8,128)(2,1)} %constant.2.clone.ends_ref), custom_call_target="tpu_custom_call" | custom-call | flops 12582912 | bytes 6291456 | tf_op jit(solution)/shard_map/own_rows/pallas_call | solution.py:316
  73.3 0.0 collective-permute-done.6.rzy_ref
  73.3 0.1 pad_maximum_fusion.2
  73.4 0.2 collective-permute-done.5.ry_ref
  73.6 1.0 %fusion.1 = f32[1,4,8,8,128]{4,3,2,1,0:T(8,128)S(1)} fusion(f32[1,4,8,8,128]{4,3,2,1,0:T(8,128)} %get-tuple-element.23, f32[1,4,1,8,128]{4,3,2,1,0:T(8,128)S(1)} %get-tuple-element.33, f32[1,4,1,8,128]{4,3,2,1,0:T(8,128)S(1)} %get-tuple-element.32, f32[1,1,8,8,128]{4,3,2,1,0:T(8,128)S(1)} %get-tuple-element.29, ...), kind=kLoop, calls=%fused_computation.3 | loop fusion | flops 294912 | bytes 426032 | tf_op jit(solution)/shard_map/add | solution.py:415
  74.7 2.0 %collective-permute-start.7 = (f32[1,4,8,8,128]{4,3,2,1,0:T(8,128)S(1)}, f32[1,4,8,8,128]{4,3,2,1,0:T(8,128)S(1)}, u32[]{:S(2)}, u32[]{:S(2)}) collective-permute-start(f32[1,4,8,8,128]{4,3,2,1,0:T(8,128)S(1)} %fusion.1), channel_id=1, source_target_pairs={{12,0},{13,1},{14,2},{15,3},{0,4},{1,5},{2,6},{3,7},{4,8},{5,9},{6... | collective-permute-start | bytes 393224 | tf_op jit(solution)/shard_map/ppermute | solution.py:33
  76.7 0.0 collective-permute-start.8
  76.7 2.4 %collective-permute-start.9 = (f32[1,128]{1,0:T(1,128)S(1)}, f32[1,128]{1,0:T(1,128)S(1)}, u32[]{:S(2)}, u32[]{:S(2)}) collective-permute-start(f32[1,128]{1,0:T(1,128)S(1)} %slice_bitcast_fusion), channel_id=1, source_target_pairs={{4,0},{5,1},{6,2},{7,3},{8,4},{9,5},{10,6},{11,7},{12,8},{13,9},{1... | collective-permute-start | bytes 1544 | tf_op jit(solution)/shard_map/ppermute | solution.py:33
  79.1 2.0 %collective-permute-done.8.refs_0_ = f32[1,128]{1,0:T(1,128)S(1)} collective-permute-done((f32[1,128]{1,0:T(1,128)S(1)}, f32[1,128]{1,0:T(1,128)S(1)}, u32[]{:S(2)}, u32[]{:S(2)}) %collective-permute-start.8) | collective-permute-done | bytes 544 | tf_op jit(solution)/shard_map/ppermute | solution.py:33
  81.2 0.7 collective-permute-done.7.rx_ref
  81.9 0.6 copy-done.4
  82.6 1.7 %join_forces.1 = (f32[1,4,3,8,128]{4,3,2,1,0:T(8,128)}, f32[1,128]{1,0:T(1,128)}) custom-call(f32[1,4,8,8,128]{4,3,2,1,0:T(8,128)} %own_rows.1.own_ref, f32[2,4,2,8,128]{4,3,2,1,0:T(8,128)} %copy-done.2, f32[2,2,8,8,128]{4,3,2,1,0:T(8,128)} %copy-done, f32[2,2,2,8,128]{4,3,2,1,0:T(8,128)} %copy-done.6, f32[1,4,8,8,128]{4,3,2,1,0:T(8,128)} %copy-done.4, ...), custom_call_target="tpu_custom_call" | custom-call | tf_op jit(solution)/shard_map/join_forces/pallas_call | solution.py:55
  (28 shorter events, 0.1 us)
Async XLA Ops:
  2.2 1.6 %collective-permute-start = (f32[1,4,2,8,128]{4,3,2,1,0:T(8,128)}, f32[1,4,2,8,128]{4,3,2,1,0:T(8,128)S(1)}, u32[]{:S(2)}, u32[]{:S(2)}) collective-permute-start(f32[1,4,2,8,128]{4,3,2,1,0:T(8,128)} %get-tuple-element.15), channel_id=1, source_target_pairs={{1,0},{0,1},{3,2},{2,3},{5,4},{4,5},{7,6},{6,7},{9,8},{8,9},{11,10... | collective-permute-start | bytes 98312 | tf_op jit(solution)/shard_map/ppermute | solution.py:33
  3.8 16.4 %copy-start.3 = (f32[1,4,2,8,128]{4,3,2,1,0:T(8,128)}, f32[1,4,2,8,128]{4,3,2,1,0:T(8,128)S(1)}, u32[]{:S(2)}) copy-start(f32[1,4,2,8,128]{4,3,2,1,0:T(8,128)S(1)} %collective-permute-done.pz_ref) | copy-start | bytes 98308
  4.7 15.4 %collective-permute-start.2 = (f32[1,4,10,8,128]{4,3,2,1,0:T(8,128)S(1)}, f32[1,4,10,8,128]{4,3,2,1,0:T(8,128)S(1)}, u32[]{:S(2)}, u32[]{:S(2)}) collective-permute-start(f32[1,4,10,8,128]{4,3,2,1,0:T(8,128)S(1)} %pad_maximum_fusion), channel_id=1, source_target_pairs={{4,0},{5,1},{6,2},{7,3},{8,4},{9,5},{10,6},{11,7},{12,8},{13,9},{1... | collective-permute-start | bytes 491528 | tf_op jit(solution)/shard_map/ppermute | solution.py:33
  9.7 10.4 %collective-permute-start.3 = (f32[1,2,10,8,128]{4,3,2,1,0:T(8,128)S(1)}, f32[1,2,10,8,128]{4,3,2,1,0:T(8,128)S(1)}, u32[]{:S(2)}, u32[]{:S(2)}) collective-permute-start(f32[1,2,10,8,128]{4,3,2,1,0:T(8,128)S(1)} %pad_maximum_fusion.1), channel_id=1, source_target_pairs={{6,0},{7,1},{4,2},{5,3},{10,4},{11,5},{8,6},{9,7},{14,8},{15,9},{1... | collective-permute-start | bytes 245768 | tf_op jit(solution)/shard_map/ppermute | solution.py:33
  11.1 9.0 %collective-permute-start.1 = (f32[1,1,10,8,128]{4,3,2,1,0:T(8,128)S(1)}, f32[1,1,10,8,128]{4,3,2,1,0:T(8,128)S(1)}, u32[]{:S(2)}, u32[]{:S(2)}) collective-permute-start(f32[1,1,10,8,128]{4,3,2,1,0:T(8,128)S(1)} %get-tuple-element.27), channel_id=1, source_target_pairs={{2,0},{3,1},{0,2},{1,3},{6,4},{7,5},{4,6},{5,7},{10,8},{11,9},{8,1... | collective-permute-start | bytes 122888 | tf_op jit(solution)/shard_map/ppermute | solution.py:33
  20.1 0.6 copy-start.7
  20.1 0.6 copy-start.5
  20.8 0.7 copy-start.1
  64.9 8.4 %collective-permute-start.6 = (f32[2,2,2,8,128]{4,3,2,1,0:T(8,128)}, f32[2,2,2,8,128]{4,3,2,1,0:T(8,128)S(1)}, u32[]{:S(2)}, u32[]{:S(2)}) collective-permute-start(f32[2,2,2,8,128]{4,3,2,1,0:T(8,128)} %get-tuple-element.22), channel_id=1, source_target_pairs={{3,0},{2,1},{1,2},{0,3},{7,4},{6,5},{5,6},{4,7},{11,8},{10,9},{9,1... | collective-permute-start | bytes 98312 | tf_op jit(solution)/shard_map/ppermute | solution.py:33
  67.5 5.9 %collective-permute-start.4 = (f32[2,4,2,8,128]{4,3,2,1,0:T(8,128)}, f32[2,4,2,8,128]{4,3,2,1,0:T(8,128)S(1)}, u32[]{:S(2)}, u32[]{:S(2)}) collective-permute-start(f32[2,4,2,8,128]{4,3,2,1,0:T(8,128)} %get-tuple-element.18), channel_id=1, source_target_pairs={{1,0},{0,1},{3,2},{2,3},{5,4},{4,5},{7,6},{6,7},{9,8},{8,9},{11,10... | collective-permute-start | bytes 196616 | tf_op jit(solution)/shard_map/ppermute | solution.py:33
  67.5 6.1 %collective-permute-start.5 = (f32[2,2,8,8,128]{4,3,2,1,0:T(8,128)}, f32[2,2,8,8,128]{4,3,2,1,0:T(8,128)S(1)}, u32[]{:S(2)}, u32[]{:S(2)}) collective-permute-start(f32[2,2,8,8,128]{4,3,2,1,0:T(8,128)} %get-tuple-element.21), channel_id=1, source_target_pairs={{2,0},{3,1},{0,2},{1,3},{6,4},{7,5},{4,6},{5,7},{10,8},{11,9},{8,1... | collective-permute-start | bytes 393224 | tf_op jit(solution)/shard_map/ppermute | solution.py:33
  73.3 8.6 %copy-start.6 = (f32[2,2,2,8,128]{4,3,2,1,0:T(8,128)}, f32[2,2,2,8,128]{4,3,2,1,0:T(8,128)S(1)}, u32[]{:S(2)}) copy-start(f32[2,2,2,8,128]{4,3,2,1,0:T(8,128)S(1)} %collective-permute-done.6.rzy_ref) | copy-start | bytes 98308
  73.4 8.5 %copy-start.2 = (f32[2,4,2,8,128]{4,3,2,1,0:T(8,128)}, f32[2,4,2,8,128]{4,3,2,1,0:T(8,128)S(1)}, u32[]{:S(2)}) copy-start(f32[2,4,2,8,128]{4,3,2,1,0:T(8,128)S(1)} %collective-permute-done.4.rz_ref) | copy-start | bytes 196612
  73.6 8.3 %copy-start = (f32[2,2,8,8,128]{4,3,2,1,0:T(8,128)}, f32[2,2,8,8,128]{4,3,2,1,0:T(8,128)S(1)}, u32[]{:S(2)}) copy-start(f32[2,2,8,8,128]{4,3,2,1,0:T(8,128)S(1)} %collective-permute-done.5.ry_ref) | copy-start | bytes 393220
  74.7 7.2 %collective-permute-start.7 = (f32[1,4,8,8,128]{4,3,2,1,0:T(8,128)S(1)}, f32[1,4,8,8,128]{4,3,2,1,0:T(8,128)S(1)}, u32[]{:S(2)}, u32[]{:S(2)}) collective-permute-start(f32[1,4,8,8,128]{4,3,2,1,0:T(8,128)S(1)} %fusion.1), channel_id=1, source_target_pairs={{12,0},{13,1},{14,2},{15,3},{0,4},{1,5},{2,6},{3,7},{4,8},{5,9},{6... | collective-permute-start | bytes 393224 | tf_op jit(solution)/shard_map/ppermute | solution.py:33
  76.7 4.5 %collective-permute-start.8 = (f32[1,128]{1,0:T(1,128)S(1)}, f32[1,128]{1,0:T(1,128)S(1)}, u32[]{:S(2)}, u32[]{:S(2)}) collective-permute-start(f32[1,128]{1,0:T(1,128)S(1)} %slice_bitcast_fusion), channel_id=1, source_target_pairs={{8,0},{9,1},{10,2},{11,3},{12,4},{13,5},{14,6},{15,7},{0,8},{1,9},... | collective-permute-start | bytes 1544 | tf_op jit(solution)/shard_map/ppermute | solution.py:33
  76.7 4.5 %collective-permute-start.9 = (f32[1,128]{1,0:T(1,128)S(1)}, f32[1,128]{1,0:T(1,128)S(1)}, u32[]{:S(2)}, u32[]{:S(2)}) collective-permute-start(f32[1,128]{1,0:T(1,128)S(1)} %slice_bitcast_fusion), channel_id=1, source_target_pairs={{4,0},{5,1},{6,2},{7,3},{8,4},{9,5},{10,6},{11,7},{12,8},{13,9},{1... | collective-permute-start | bytes 1544 | tf_op jit(solution)/shard_map/ppermute | solution.py:33
  81.1 0.8 copy-start.8
  81.2 0.8 copy-start.9
  81.9 0.6 copy-start.4

commit v2 on v1

--- a/solution.py
+++ b/solution.py
@@ -15,7 +15,6 @@
 K3 = EDGE_T**-3.0
 K6 = EDGE_T**-6.0
 OFFSETS = (
-    (0, 0, 0),
     (0, 0, 1),
     (0, 1, 0),
     (0, 1, 1),
@@ -61,37 +60,101 @@
     )(*operands)
 
 
-def row_kernel(packed_ref, c6_ref, c12_ref, left_ref, rows_ref, table_ref):
-    cells_z, _, slots = packed_ref.shape[2:]
+def pair_terms(dx, dy, dz, qq, c6, c12, kept=None):
+    t = dx * dx + dy * dy + (dz * dz + SOFTEN)
+    y = lax.rsqrt(t)
+    v = y * y
+    v3 = v * v * v
+    p = qq * y
+    h = c12 * v3
+    m = h - c6
+    gap = v3 - K3
+    u = qq * (y - K1) + gap * m
+    z = p + (6.0 * v3) * (m + c12 * gap)
+    w = jnp.maximum(EDGE_T - t, 0.0)
+    if kept is not None:
+        w = jnp.where(kept, w, 0.0)
+    return w * ((w * v) * z + 4.0 * u), w * (w * u)
+
+
+def row_kernel(packed_ref, c6_ref, c12_ref, left_ref, rows_hbm, self_ref, energy_ref, table_ref, rows_ref, sem):
+    cells_x, cells_y, cells_z, _, slots = packed_ref.shape
     f32, bf16 = jnp.float32, jnp.bfloat16
     row_id = lax.broadcasted_iota(jnp.int32, (8, slots), 0)
-    lane_of = lax.broadcasted_iota(jnp.int32, (slots, slots), 1).astype(f32)
-    ix, iy = pl.program_id(0), pl.program_id(1) + 1
-
-    @pl.when((pl.program_id(0) == 0) & (pl.program_id(1) == 0))
-    def _():
-        kinds = c6_ref.shape[0]
-        table_ref[...] = jnp.zeros_like(table_ref)
-        c6, c12 = ((0.5 * ENERGY_UNIT) * (c[...] + c[...].T) for c in (c6_ref, c12_ref))
-        for k, table in enumerate((c6 - c12 * K3, c12)):
-            high = table.astype(bf16)
-            at = slice(k * slots, k * slots + kinds)
-            table_ref[0:kinds, at] = high
-            table_ref[slots : slots + kinds, at] = (table - high.astype(f32)).astype(bf16)
-
-    for iz in range(cells_z):
-        at = jnp.where(row_id == 0, ix, jnp.where(row_id == 1, iy, jnp.where(row_id == 2, iz + 1, 0)))
-        f = packed_ref[0, 0, iz] + at.astype(f32) * CELL_EDGE
-        high = f.astype(bf16).astype(f32)
-        mid = (f - high).astype(bf16).astype(f32)
-        parts = jnp.concatenate([high, mid, f - high - mid], axis=0).T.astype(bf16)
-        mine = jnp.dot(parts, left_ref[...], preferred_element_type=f32)
-        hot = (mine[:, 4 * slots :] == lane_of).astype(f32).astype(bf16)
+    lane = lax.broadcasted_iota(jnp.int32, (8, slots), 1)
+    lane_of = lax.broadcasted_iota(jnp.int32, (cells_z * slots, slots), 1).astype(f32)
+    lines = cells_x * cells_y
+
+    kinds = c6_ref.shape[0]
+    table_ref[...] = jnp.zeros_like(table_ref)
+    c6, c12 = ((0.5 * ENERGY_UNIT) * (c[...] + c[...].T) for c in (c6_ref, c12_ref))
+    for k, table in enumerate((c6 - c12 * K3, c12)):
+        high = table.astype(bf16)
+        at = slice(k * slots, k * slots + kinds)
+        table_ref[0:kinds, at] = high
+        table_ref[slots : slots + kinds, at] = (table - high.astype(f32)).astype(bf16)
+
+    def store(line):
+        slot = line % 2
+        return pltpu.make_async_copy(rows_ref.at[slot], rows_hbm.at[line], sem.at[slot])
+
+    def do_line(line, energy):
+        ix, iy, slot = line // cells_y, line % cells_y, line % 2
+
+        def placed(iz):
+            at = jnp.where(row_id == 0, ix, jnp.where(row_id == 1, iy + 1, jnp.where(row_id == 2, iz + 1, 0)))
+            return packed_ref[ix, iy, iz] + at.astype(f32) * CELL_EDGE
+
+        @pl.when(line >= 2)
+        def _():
+            store(line - 2).wait()
+
+        def split(iz):
+            f = placed(iz)
+            high = f.astype(bf16).astype(f32)
+            mid = (f - high).astype(bf16).astype(f32)
+            return jnp.concatenate([high, mid, f - high - mid], axis=0).T.astype(bf16)
+
+        parts = jnp.concatenate([split(iz) for iz in range(cells_z)], axis=0)
+        cut = lambda product, k: product[:, k * slots : (k + 1) * slots].reshape(cells_z, slots, slots)
+        kinds_of = jnp.dot(parts, left_ref[:, 4 * slots :], preferred_element_type=f32)
+        hot = (kinds_of == lane_of).astype(f32).astype(bf16)
+        for first in (0, 2):
+            mine = jnp.dot(
+                parts, left_ref[:, first * slots : (first + 2) * slots], preferred_element_type=f32
+            )
+            for k in range(2):
+                rows_ref[slot, :, first + k] = cut(mine, k)
         looked = jnp.dot(jnp.concatenate([hot, hot], axis=1), table_ref[...], preferred_element_type=f32)
-        for k in range(4):
-            rows_ref[0, iz, k] = mine[:, k * slots : (k + 1) * slots]
         for k in range(2):
-            rows_ref[0, iz, 4 + k] = looked[:, k * slots : (k + 1) * slots]
+            rows_ref[slot, :, 4 + k] = cut(looked, k)
+        store(line).start()
+
+        def inside(iz, energy):
+            f = placed(iz)
+            bx, by, bz, bq = (jnp.broadcast_to(f[k : k + 1], (8, slots)) for k in range(4))
+            kind = jnp.broadcast_to(f[4:5].astype(jnp.int32), (8, slots))
+            fold = None
+            for at in range(0, slots, 8):
+                ax, ay, az, aq, a6, a12 = (rows_ref[slot, iz, k, at : at + 8, :] for k in range(6))
+                dx, dy, dz = bx - ax, by - ay, bz - az
+                c6, c12 = (
+                    jnp.take_along_axis(t, kind, axis=1, mode="promise_in_bounds") for t in (a6, a12)
+                )
+                s, e = pair_terms(dx, dy, dz, bq * aq, c6, c12, lane != row_id + at)
+                energy = energy + e
+                moved = (s * dx, s * dy, s * dz)
+                fold = moved if fold is None else tuple(a + b for a, b in zip(fold, moved))
+            for k in range(3):
+                self_ref[line, iz, k] = fold[k]
+            return energy
+
+        return lax.fori_loop(0, cells_z, inside, energy)
+
+    energy = lax.fori_loop(0, lines, do_line, jnp.zeros((8, slots), f32))
+    energy_ref[...] = 0.5 * energy
+    for line in range(max(lines - 2, 0), lines):
+        store(line).wait()
 
 
 def row_call(packed, c6_table, c12_table):
@@ -102,18 +165,22 @@
             left[8 * n + k, k * slots : (k + 1) * slots] = 1.0
     left = jnp.asarray(left, jnp.bfloat16)
     atoms = cells_x * cells_y * cells_z * slots
+    line = (cells_z, 6, slots, slots)
+    vmem = pl.BlockSpec(memory_space=pltpu.VMEM)
     return pl.pallas_call(
         row_kernel,
-        grid=(cells_x, cells_y),
-        out_shape=jax.ShapeDtypeStruct((cells_x * cells_y, cells_z, 6, slots, slots), jnp.float32),
-        in_specs=[
-            pl.BlockSpec((1, 1, cells_z, 8, slots), lambda i, j: (i, j, 0, 0, 0)),
-            pl.BlockSpec(c6_table.shape, lambda i, j: (0, 0)),
-            pl.BlockSpec(c12_table.shape, lambda i, j: (0, 0)),
-            pl.BlockSpec(left.shape, lambda i, j: (0, 0)),
+        out_shape=(
+            jax.ShapeDtypeStruct((cells_x * cells_y,) + line, jnp.float32),
+            jax.ShapeDtypeStruct((cells_x * cells_y, cells_z, 3, 8, slots), jnp.float32),
+            jax.ShapeDtypeStruct((8, slots), jnp.float32),
+        ),
+        in_specs=[vmem] * 4,
+        out_specs=(pl.BlockSpec(memory_space=pl.ANY), vmem, vmem),
+        scratch_shapes=[
+            pltpu.VMEM((2 * slots, 2 * slots), jnp.bfloat16),
+            pltpu.VMEM((2,) + line, jnp.float32),
+            pltpu.SemaphoreType.DMA((2,)),
         ],
-        out_specs=pl.BlockSpec((1, cells_z, 6, slots, slots), lambda i, j: (i * cells_y + j, 0, 0, 0, 0)),
-        scratch_shapes=[pltpu.VMEM((2 * slots, 2 * slots), jnp.bfloat16)],
         cost_estimate=pl.CostEstimate(
             flops=2 * atoms * slots * 376, transcendentals=0, bytes_accessed=atoms * slots * 24
         ),
@@ -122,7 +189,7 @@
 
 
 def pair_kernel(
-    counts_ref, packed_ref, pz_ref, py_ref, px_ref, pc_ref, rows_ref,
+    counts_ref, packed_ref, pz_ref, py_ref, px_ref, pc_ref, self_ref, energy_ref, rows_ref,
     own_ref, oz_ref, oy_ref, ozy_ref, ox_ref, fa,
     fe, types, fb, eacc,
 ):
@@ -134,7 +201,7 @@
 
     @pl.when(line == 0)
     def _():
-        eacc[...] = jnp.zeros_like(eacc)
+        eacc[...] = energy_ref[...]
 
         def place(f, ix, iy, iz):
             at = jnp.where(row_id == 0, ix, jnp.where(row_id == 1, iy, jnp.where(row_id == 2, iz, 0)))
@@ -146,6 +213,7 @@
             for ix in range(cells_x):
                 for iz in range(cells_z):
                     place(packed_ref[ix, iy, iz], ix, iy + 1, iz + 1)
+                    fb[ix, iy + 1, iz + 1] = self_ref[ix * cells_y + iy, iz]
                 place(pz_ref[ix, iy, 0], ix, iy + 1, cells_z + 1)
                 place(pz_ref[ix, iy, 1], ix, iy + 1, 0)
             for iz in range(ext_z):
@@ -183,23 +251,7 @@
                 c6, c12 = (
                     jnp.take_along_axis(t, kind, axis=1, mode="promise_in_bounds") for t in (a6, a12)
                 )
-                t = dx * dx + dy * dy + (dz * dz + SOFTEN)
-                y = lax.rsqrt(t)
-                v = y * y
-                v3 = v * v * v
-                p = qq * y
-                h = c12 * v3
-                m = h - c6
-                gap = v3 - K3
-                u = qq * (y - K1) + gap * m
-                z = p + (6.0 * v3) * (m + c12 * gap)
-                w = jnp.maximum(EDGE_T - t, 0.0)
-                if (ox, oy, oz) == (0, 0, 0):
-                    lane = lax.broadcasted_iota(jnp.int32, (rows, slots), 1)
-                    row = lax.broadcasted_iota(jnp.int32, (rows, slots), 0) + at
-                    w = jnp.where(lane > row, w, 0.0)
-                s = w * ((w * v) * z + 4.0 * u)
-                e = w * (w * u)
+                s, e = pair_terms(dx, dy, dz, qq, c6, c12)
                 for r in range(0, rows, 8):
                     energy = energy + e[r : r + 8]
                 px, py, pz = s * dx, s * dy, s * dz
@@ -258,7 +310,7 @@
                     ozy_ref[ix, a, b] = total_of(ix, at_y, at_z)
 
 
-def pair_call(counts, pieces, rows):
+def pair_call(counts, pieces, rows, inside, energy):
     cells_x, cells_y, cells_z = counts.shape
     slots = rows.shape[-1]
     f32 = jnp.float32
@@ -281,7 +333,7 @@
         grid=(cells_x * cells_y,),
         out_shape=tuple(jax.ShapeDtypeStruct(o, f32) for o in outs + [sums]),
         in_specs=[pl.BlockSpec(memory_space=pltpu.SMEM)]
-        + [fixed(piece.shape) for piece in pieces]
+        + [fixed(piece.shape) for piece in (*pieces, inside, energy)]
         + [by_line(rows.shape)],
         out_specs=tuple(fixed(o) for o in outs) + (by_line(sums),),
         scratch_shapes=[
@@ -291,7 +343,7 @@
             pltpu.VMEM((8, slots), f32),
         ],
         name="pair_forces",
-    )(counts, *pieces, rows)
+    )(counts, *pieces, inside, energy, rows)
 
 
 def own_kernel(sums_ref, own_ref, ends_ref, out_ref):
@@ -407,8 +459,10 @@
         pc = moved(ends, -1, -1, 0)
     else:
         pc = jnp.concatenate([moved(ends[:, :1], -1, -1, 0), moved(ends[:, 1:], -1, 1, 0)], axis=1)
-    rows = row_call(packed, c6_table, c12_table)
-    own, oz, oy, ozy, ox, sums = pair_call(counts, (packed, pz, py, px, pc), rows)
+    rows, inside, within = row_call(packed, c6_table, c12_table)
+    own, oz, oy, ozy, ox, sums = pair_call(
+        counts, (packed, pz, py, px, pc), rows, inside, within
+    )
     rz, ry, rzy = to_sides(oz, oy, ozy, ny, nz)
     own, rz = lax.optimization_barrier((own_call(sums, own), rz))
     ox = (

time: 85.9 us -> 83 us (0.966)
  Pallas kernels: 60.7 us -> 57.5 us
  starting transfers between devices: 14.6 us -> 15.9 us
    pallas_call x1, Pallas kernels: 43.5 us -> 39.1 us  [pair_call(): pl.pallas_call(pair_kernel, grid=(cells_x * cells_y,), out_shape=tuple((j...]
    ppermute x10, starting transfers between devices: 14.6 us -> 15.9 us  [moved(): return lax.ppermute(block, AXES, route)]
    pallas_call x1, Pallas kernels: 8.49 us -> 9.7 us  [row_call(): pl.pallas_call(row_kernel, out_shape=(jax.ShapeDtypeStruct((cells_x * cel...]
  transfers between devices with their start and end apart: 10 -> 10, of which waited for: 4 -> 4; matrix products, arithmetic and copies ran while one was open for 0% -> 0% of each run, Pallas kernels for 16% -> 18%
where the time goes in v2:
time: 83 us; the launch traced here: 81.6 us
  Pallas kernels  57.5 us (69%)
  starting transfers between devices  15.9 us (19%)
  waiting for transfers between devices  3.61 us (4%)
  other arithmetic  2.06 us (2%)
  local copies, waits for them, and re-layouts  1.75 us (2%)
    pallas_call x1, Pallas kernels, pair_call(): pl.pallas_call(pair_kernel, grid=(cells_x * cells_y,), out_shape=tuple((j...  39.1 us
    ppermute x10, starting transfers between devices, moved(): return lax.ppermute(block, AXES, route)  15.9 us
    pallas_call x1, Pallas kernels, row_call(): pl.pallas_call(row_kernel, out_shape=(jax.ShapeDtypeStruct((cells_x * cel...  9.7 us
    pallas_call x1, Pallas kernels, own_call(): pl.pallas_call(own_kernel, grid=(cells_x, cells_y), out_shape=jax.ShapeDt...  5.38 us
    ppermute x10, waiting for transfers between devices, moved(): return lax.ppermute(block, AXES, route)  3.61 us
    pallas_call x2, Pallas kernels, whole_call(): pl.pallas_call(kernel, out_shape=tuple((jax.ShapeDtypeStruct(o, jnp.float...  3.3 us
  transfers between devices with their start and end apart: 10, of which 4 were waited for; matrix products, arithmetic and copies ran while one was open for 0% of the time, Pallas kernels for 18%

profile of v2, /device:TPU:0, one launch (start us, length us, event | category | flops | bytes accessed | tf_op | source)
XLA Modules:
  0.0 81.6 jit_solution(1174857679353700437)
XLA Ops:
  0.6 1.6 %pack_cells.1 = (f32[1,4,8,8,128]{4,3,2,1,0:T(8,128)}, f32[1,4,2,8,128]{4,3,2,1,0:T(8,128)}) custom-call(s32[1,4,8]{2,1,0:T(4,128)} %counts_ref.3, f32[1,4,3,8,128]{4,3,2,1,0:T(8,128)} %bitcast.6, f32[1,4,8,128]{3,2,1,0:T(8,128)} %charges_ref.1, s32[1,4,8,128]{3,2,1,0:T(8,128)} %types_ref.1), custom_call_target="tpu_custom_call" | custom-call | tf_op jit(solution)/shard_map/pack_cells/pallas_call | solution.py:54
  2.2 0.5 collective-permute-start
  2.7 1.1 %collective-permute-done.pz_ref = f32[1,4,2,8,128]{4,3,2,1,0:T(8,128)S(1)} collective-permute-done((f32[1,4,2,8,128]{4,3,2,1,0:T(8,128)}, f32[1,4,2,8,128]{4,3,2,1,0:T(8,128)S(1)}, u32[]{:S(2)}, u32[]{:S(2)}) %collective-permute-start) | collective-permute-done | bytes 32800 | tf_op jit(solution)/shard_map/ppermute | solution.py:32
  3.8 0.9 %pad_maximum_fusion = f32[1,4,10,8,128]{4,3,2,1,0:T(8,128)S(1)} fusion(f32[1,4,1,8,128]{4,3,2,1,0:T(8,128)S(1)} %get-tuple-element.43, f32[1,4,8,8,128]{4,3,2,1,0:T(8,128)} %get-tuple-element.17.packed_ref, f32[1,4,1,8,128]{4,3,2,1,0:T(8,128)S(1)} %get-tuple-element.42), kind=kLoop, calls=%fused_computation | loop fusion | flops 81920 | bytes 327680 | tf_op jit(solution)/shard_map/concatenate | solution.py:454
  4.7 5.0 %collective-permute-start.2 = (f32[1,4,10,8,128]{4,3,2,1,0:T(8,128)S(1)}, f32[1,4,10,8,128]{4,3,2,1,0:T(8,128)S(1)}, u32[]{:S(2)}, u32[]{:S(2)}) collective-permute-start(f32[1,4,10,8,128]{4,3,2,1,0:T(8,128)S(1)} %pad_maximum_fusion), channel_id=1, source_target_pairs={{4,0},{5,1},{6,2},{7,3},{8,4},{9,5},{10,6},{11,7},{12,8},{13,9},{1... | collective-permute-start | bytes 491528 | tf_op jit(solution)/shard_map/ppermute | solution.py:32
  9.7 1.4 %collective-permute-start.3 = (f32[1,2,10,8,128]{4,3,2,1,0:T(8,128)S(1)}, f32[1,2,10,8,128]{4,3,2,1,0:T(8,128)S(1)}, u32[]{:S(2)}, u32[]{:S(2)}) collective-permute-start(f32[1,2,10,8,128]{4,3,2,1,0:T(8,128)S(1)} %pad_maximum_fusion.1), channel_id=1, source_target_pairs={{6,0},{7,1},{4,2},{5,3},{10,4},{11,5},{8,6},{9,7},{14,8},{15,9},{1... | collective-permute-start | bytes 245768 | tf_op jit(solution)/shard_map/ppermute | solution.py:32
  11.1 0.5 collective-permute-start.1
  11.6 9.7 %row_operands.1 = (f32[4,8,6,128,128]{4,3,2,1,0:T(8,128)}, f32[4,8,3,8,128]{4,3,2,1,0:T(8,128)}, f32[8,128]{1,0:T(8,128)}) custom-call(f32[1,4,8,8,128]{4,3,2,1,0:T(8,128)} %get-tuple-element.17.packed_ref, f32[64,64]{1,0:T(8,128)} %c6_ref.1, f32[64,64]{1,0:T(8,128)} %c12_ref.1, bf16[24,640]{1,0:T(8,128)(2,1)} %constant.4.clone.left_ref), custom_call_target="tpu_custom_call" | custom-call | flops 394264576 | bytes 12582912 | tf_op jit(solution)/shard_map/row_operands/pallas_call | solution.py:170
  21.3 0.0 copy-start.7
  21.3 0.0 collective-permute-done.3.pc_ref
  21.4 0.6 copy-done.7
  22.0 0.0 copy-done.5
  22.0 0.1 copy-done.1
  22.1 39.1 %pair_forces.1 = (f32[1,4,8,8,128]{4,3,2,1,0:T(8,128)}, f32[2,4,2,8,128]{4,3,2,1,0:T(8,128)}, f32[2,2,8,8,128]{4,3,2,1,0:T(8,128)}, f32[2,2,2,8,128]{4,3,2,1,0:T...) custom-call(s32[1,4,8]{2,1,0:T(4,128)} %counts_ref.3, ...), custom_call_target="tpu_custom_call" | custom-call | tf_op jit(solution)/shard_map/pair_forces/pallas_call | solution.py:331
  61.2 1.8 %collective-permute-start.6 = (f32[2,2,2,8,128]{4,3,2,1,0:T(8,128)}, f32[2,2,2,8,128]{4,3,2,1,0:T(8,128)S(1)}, u32[]{:S(2)}, u32[]{:S(2)}) collective-permute-start(f32[2,2,2,8,128]{4,3,2,1,0:T(8,128)} %get-tuple-element.28), channel_id=1, source_target_pairs={{3,0},{2,1},{1,2},{0,3},{7,4},{6,5},{5,6},{4,7},{11,8},{10,9},{9,1... | collective-permute-start | bytes 98312 | tf_op jit(solution)/shard_map/ppermute | solution.py:32
  63.0 0.1 pad.10.clone
  63.1 0.1 pad.7.clone
  63.2 1.8 %collective-permute-start.4 = (f32[2,4,2,8,128]{4,3,2,1,0:T(8,128)}, f32[2,4,2,8,128]{4,3,2,1,0:T(8,128)S(1)}, u32[]{:S(2)}, u32[]{:S(2)}) collective-permute-start(f32[2,4,2,8,128]{4,3,2,1,0:T(8,128)} %get-tuple-element.24), channel_id=1, source_target_pairs={{1,0},{0,1},{3,2},{2,3},{5,4},{4,5},{7,6},{6,7},{9,8},{8,9},{11,10... | collective-permute-start | bytes 196616 | tf_op jit(solution)/shard_map/ppermute | solution.py:32
  65.0 0.0 collective-permute-start.5
  65.0 5.4 %own_rows.1.own_ref = f32[1,4,8,8,128]{4,3,2,1,0:T(8,128)} custom-call(f32[4,8,3,128,128]{4,3,2,1,0:T(8,128)} %get-tuple-element.22.sums_ref, f32[1,4,8,8,128]{4,3,2,1,0:T(8,128)} %get-tuple-element.23.own_ref, bf16[768,128]{1,0:T(8,128)(2,1)} %constant.2.clone.ends_ref), custom_call_target="tpu_custom_call" | custom-call | flops 12582912 | bytes 6291456 | tf_op jit(solution)/shard_map/own_rows/pallas_call | solution.py:368
  70.4 0.1 pad_maximum_fusion.2
  70.5 0.2 collective-permute-done.5.ry_ref
  70.7 1.0 %fusion.1 = f32[1,4,8,8,128]{4,3,2,1,0:T(8,128)S(1)} fusion(f32[1,4,8,8,128]{4,3,2,1,0:T(8,128)} %get-tuple-element.29, f32[1,4,1,8,128]{4,3,2,1,0:T(8,128)S(1)} %get-tuple-element.39, f32[1,4,1,8,128]{4,3,2,1,0:T(8,128)S(1)} %get-tuple-element.38, f32[1,1,8,8,128]{4,3,2,1,0:T(8,128)S(1)} %get-tuple-element.35, ...), kind=kLoop, calls=%fused_computation.3 | loop fusion | flops 294912 | bytes 426032 | tf_op jit(solution)/shard_map/add | solution.py:469
  71.8 2.4 %collective-permute-start.7 = (f32[1,4,8,8,128]{4,3,2,1,0:T(8,128)S(1)}, f32[1,4,8,8,128]{4,3,2,1,0:T(8,128)S(1)}, u32[]{:S(2)}, u32[]{:S(2)}) collective-permute-start(f32[1,4,8,8,128]{4,3,2,1,0:T(8,128)S(1)} %fusion.1), channel_id=1, source_target_pairs={{12,0},{13,1},{14,2},{15,3},{0,4},{1,5},{2,6},{3,7},{4,8},{5,9},{6... | collective-permute-start | bytes 393224 | tf_op jit(solution)/shard_map/ppermute | solution.py:32
  74.2 0.0 collective-permute-start.8
  74.2 2.4 %collective-permute-start.9 = (f32[1,128]{1,0:T(1,128)S(1)}, f32[1,128]{1,0:T(1,128)S(1)}, u32[]{:S(2)}, u32[]{:S(2)}) collective-permute-start(f32[1,128]{1,0:T(1,128)S(1)} %slice_bitcast_fusion), channel_id=1, source_target_pairs={{4,0},{5,1},{6,2},{7,3},{8,4},{9,5},{10,6},{11,7},{12,8},{13,9},{1... | collective-permute-start | bytes 1544 | tf_op jit(solution)/shard_map/ppermute | solution.py:32
  76.6 2.0 %collective-permute-done.8.refs_0_ = f32[1,128]{1,0:T(1,128)S(1)} collective-permute-done((f32[1,128]{1,0:T(1,128)S(1)}, f32[1,128]{1,0:T(1,128)S(1)}, u32[]{:S(2)}, u32[]{:S(2)}) %collective-permute-start.8) | collective-permute-done | bytes 544 | tf_op jit(solution)/shard_map/ppermute | solution.py:32
  78.7 0.0 collective-permute-done.9.refs_1_
  78.7 0.3 collective-permute-done.7.rx_ref
  79.0 0.2 copy-done.8
  79.3 0.6 copy-done.4
  79.9 1.7 %join_forces.1 = (f32[1,4,3,8,128]{4,3,2,1,0:T(8,128)}, f32[1,128]{1,0:T(1,128)}) custom-call(f32[1,4,8,8,128]{4,3,2,1,0:T(8,128)} %own_rows.1.own_ref, f32[2,4,2,8,128]{4,3,2,1,0:T(8,128)} %copy-done.2, f32[2,2,8,8,128]{4,3,2,1,0:T(8,128)} %copy-done, f32[2,2,2,8,128]{4,3,2,1,0:T(8,128)} %copy-done.6, f32[1,4,8,8,128]{4,3,2,1,0:T(8,128)} %copy-done.4, ...), custom_call_target="tpu_custom_call" | custom-call | tf_op jit(solution)/shard_map/join_forces/pallas_call | solution.py:54
  (28 shorter events, 0.1 us)
Async XLA Ops:
  2.2 1.6 %collective-permute-start = (f32[1,4,2,8,128]{4,3,2,1,0:T(8,128)}, f32[1,4,2,8,128]{4,3,2,1,0:T(8,128)S(1)}, u32[]{:S(2)}, u32[]{:S(2)}) collective-permute-start(f32[1,4,2,8,128]{4,3,2,1,0:T(8,128)} %get-tuple-element.18), channel_id=1, source_target_pairs={{1,0},{0,1},{3,2},{2,3},{5,4},{4,5},{7,6},{6,7},{9,8},{8,9},{11,10... | collective-permute-start | bytes 98312 | tf_op jit(solution)/shard_map/ppermute | solution.py:32
  3.7 17.6 %copy-start.3 = (f32[1,4,2,8,128]{4,3,2,1,0:T(8,128)}, f32[1,4,2,8,128]{4,3,2,1,0:T(8,128)S(1)}, u32[]{:S(2)}) copy-start(f32[1,4,2,8,128]{4,3,2,1,0:T(8,128)S(1)} %collective-permute-done.pz_ref) | copy-start | bytes 98308
  4.7 16.7 %collective-permute-start.2 = (f32[1,4,10,8,128]{4,3,2,1,0:T(8,128)S(1)}, f32[1,4,10,8,128]{4,3,2,1,0:T(8,128)S(1)}, u32[]{:S(2)}, u32[]{:S(2)}) collective-permute-start(f32[1,4,10,8,128]{4,3,2,1,0:T(8,128)S(1)} %pad_maximum_fusion), channel_id=1, source_target_pairs={{4,0},{5,1},{6,2},{7,3},{8,4},{9,5},{10,6},{11,7},{12,8},{13,9},{1... | collective-permute-start | bytes 491528 | tf_op jit(solution)/shard_map/ppermute | solution.py:32
  9.7 11.7 %collective-permute-start.3 = (f32[1,2,10,8,128]{4,3,2,1,0:T(8,128)S(1)}, f32[1,2,10,8,128]{4,3,2,1,0:T(8,128)S(1)}, u32[]{:S(2)}, u32[]{:S(2)}) collective-permute-start(f32[1,2,10,8,128]{4,3,2,1,0:T(8,128)S(1)} %pad_maximum_fusion.1), channel_id=1, source_target_pairs={{6,0},{7,1},{4,2},{5,3},{10,4},{11,5},{8,6},{9,7},{14,8},{15,9},{1... | collective-permute-start | bytes 245768 | tf_op jit(solution)/shard_map/ppermute | solution.py:32
  11.1 10.3 %collective-permute-start.1 = (f32[1,1,10,8,128]{4,3,2,1,0:T(8,128)S(1)}, f32[1,1,10,8,128]{4,3,2,1,0:T(8,128)S(1)}, u32[]{:S(2)}, u32[]{:S(2)}) collective-permute-start(f32[1,1,10,8,128]{4,3,2,1,0:T(8,128)S(1)} %get-tuple-element.33), channel_id=1, source_target_pairs={{2,0},{3,1},{0,2},{1,3},{6,4},{7,5},{4,6},{5,7},{10,8},{11,9},{8,1... | collective-permute-start | bytes 122888 | tf_op jit(solution)/shard_map/ppermute | solution.py:32
  21.3 0.6 copy-start.7
  21.4 0.6 copy-start.5
  21.4 0.7 copy-start.1
  61.2 9.2 %collective-permute-start.6 = (f32[2,2,2,8,128]{4,3,2,1,0:T(8,128)}, f32[2,2,2,8,128]{4,3,2,1,0:T(8,128)S(1)}, u32[]{:S(2)}, u32[]{:S(2)}) collective-permute-start(f32[2,2,2,8,128]{4,3,2,1,0:T(8,128)} %get-tuple-element.28), channel_id=1, source_target_pairs={{3,0},{2,1},{1,2},{0,3},{7,4},{6,5},{5,6},{4,7},{11,8},{10,9},{9,1... | collective-permute-start | bytes 98312 | tf_op jit(solution)/shard_map/ppermute | solution.py:32
  63.2 7.3 %collective-permute-start.4 = (f32[2,4,2,8,128]{4,3,2,1,0:T(8,128)}, f32[2,4,2,8,128]{4,3,2,1,0:T(8,128)S(1)}, u32[]{:S(2)}, u32[]{:S(2)}) collective-permute-start(f32[2,4,2,8,128]{4,3,2,1,0:T(8,128)} %get-tuple-element.24), channel_id=1, source_target_pairs={{1,0},{0,1},{3,2},{2,3},{5,4},{4,5},{7,6},{6,7},{9,8},{8,9},{11,10... | collective-permute-start | bytes 196616 | tf_op jit(solution)/shard_map/ppermute | solution.py:32
  65.0 5.7 %collective-permute-start.5 = (f32[2,2,8,8,128]{4,3,2,1,0:T(8,128)}, f32[2,2,8,8,128]{4,3,2,1,0:T(8,128)S(1)}, u32[]{:S(2)}, u32[]{:S(2)}) collective-permute-start(f32[2,2,8,8,128]{4,3,2,1,0:T(8,128)} %get-tuple-element.27), channel_id=1, source_target_pairs={{2,0},{3,1},{0,2},{1,3},{6,4},{7,5},{4,6},{5,7},{10,8},{11,9},{8,1... | collective-permute-start | bytes 393224 | tf_op jit(solution)/shard_map/ppermute | solution.py:32
  70.4 8.6 %copy-start.6 = (f32[2,2,2,8,128]{4,3,2,1,0:T(8,128)}, f32[2,2,2,8,128]{4,3,2,1,0:T(8,128)S(1)}, u32[]{:S(2)}) copy-start(f32[2,2,2,8,128]{4,3,2,1,0:T(8,128)S(1)} %collective-permute-done.6.rzy_ref) | copy-start | bytes 98308
  70.5 8.5 %copy-start.2 = (f32[2,4,2,8,128]{4,3,2,1,0:T(8,128)}, f32[2,4,2,8,128]{4,3,2,1,0:T(8,128)S(1)}, u32[]{:S(2)}) copy-start(f32[2,4,2,8,128]{4,3,2,1,0:T(8,128)S(1)} %collective-permute-done.4.rz_ref) | copy-start | bytes 196612
  70.7 8.3 %copy-start = (f32[2,2,8,8,128]{4,3,2,1,0:T(8,128)}, f32[2,2,8,8,128]{4,3,2,1,0:T(8,128)S(1)}, u32[]{:S(2)}) copy-start(f32[2,2,8,8,128]{4,3,2,1,0:T(8,128)S(1)} %collective-permute-done.5.ry_ref) | copy-start | bytes 393220
  71.8 7.2 %collective-permute-start.7 = (f32[1,4,8,8,128]{4,3,2,1,0:T(8,128)S(1)}, f32[1,4,8,8,128]{4,3,2,1,0:T(8,128)S(1)}, u32[]{:S(2)}, u32[]{:S(2)}) collective-permute-start(f32[1,4,8,8,128]{4,3,2,1,0:T(8,128)S(1)} %fusion.1), channel_id=1, source_target_pairs={{12,0},{13,1},{14,2},{15,3},{0,4},{1,5},{2,6},{3,7},{4,8},{5,9},{6... | collective-permute-start | bytes 393224 | tf_op jit(solution)/shard_map/ppermute | solution.py:32
  74.2 4.5 %collective-permute-start.8 = (f32[1,128]{1,0:T(1,128)S(1)}, f32[1,128]{1,0:T(1,128)S(1)}, u32[]{:S(2)}, u32[]{:S(2)}) collective-permute-start(f32[1,128]{1,0:T(1,128)S(1)} %slice_bitcast_fusion), channel_id=1, source_target_pairs={{8,0},{9,1},{10,2},{11,3},{12,4},{13,5},{14,6},{15,7},{0,8},{1,9},... | collective-permute-start | bytes 1544 | tf_op jit(solution)/shard_map/ppermute | solution.py:32
  74.2 4.5 %collective-permute-start.9 = (f32[1,128]{1,0:T(1,128)S(1)}, f32[1,128]{1,0:T(1,128)S(1)}, u32[]{:S(2)}, u32[]{:S(2)}) collective-permute-start(f32[1,128]{1,0:T(1,128)S(1)} %slice_bitcast_fusion), channel_id=1, source_target_pairs={{4,0},{5,1},{6,2},{7,3},{8,4},{9,5},{10,6},{11,7},{12,8},{13,9},{1... | collective-permute-start | bytes 1544 | tf_op jit(solution)/shard_map/ppermute | solution.py:32
  78.7 0.6 copy-start.8
  78.7 0.6 copy-start.9
  79.3 0.7 copy-start.4

commit v3 on v2

--- a/solution.py
+++ b/solution.py
@@ -273,15 +273,19 @@
         last = full * ROWS + half * (ROWS // 2)
         eacc[...] = lax.fori_loop(0, rest, lambda c, e: chunk(last, e, ROWS // 4), energy)
 
-    ix = line // cells_y
-    iy = line % cells_y
+    share = rows_ref.shape[1]
+    steps = cells_z // share
+    ix = line // (cells_y * steps)
+    iy = line // steps % cells_y
+    low = line % steps * share
     fa[...] = jnp.zeros_like(fa)
 
-    def inner(iz, _):
-        row_cell(ix, iy, iz, iz, OFFSETS)
+    def inner(n, _):
+        row_cell(ix, iy, low + n, n, OFFSETS)
         return 0
 
-    lax.fori_loop(0, cells_z, inner, 0)
+    lax.fori_loop(0, share, inner, 0)
+
     @pl.when(line == pl.num_programs(0) - 1)
     def _():
         energy = jnp.sum(eacc[...], axis=0, keepdims=True)
@@ -325,12 +329,15 @@
             (1, cells_y, cells_z),
         )
     ]
-    sums = (cells_x * cells_y, cells_z, 3, slots, slots)
+    steps = 2 if cells_z % 2 == 0 else 1
+    lines = cells_x * cells_y
+    rows = rows.reshape((lines * steps, cells_z // steps) + rows.shape[2:])
+    sums = rows.shape[:2] + (3, slots, slots)
     by_line = lambda shape: pl.BlockSpec((1,) + shape[1:], lambda i: (i, 0, 0, 0, 0))
     grown = (cells_x + 1, cells_y + 2, cells_z + 2)
-    return pl.pallas_call(
+    *outs, sums = pl.pallas_call(
         pair_kernel,
-        grid=(cells_x * cells_y,),
+        grid=(lines * steps,),
         out_shape=tuple(jax.ShapeDtypeStruct(o, f32) for o in outs + [sums]),
         in_specs=[pl.BlockSpec(memory_space=pltpu.SMEM)]
         + [fixed(piece.shape) for piece in (*pieces, inside, energy)]
@@ -344,6 +351,7 @@
         ],
         name="pair_forces",
     )(counts, *pieces, inside, energy, rows)
+    return (*outs, sums.reshape((lines, cells_z) + sums.shape[2:]))
 
 
 def own_kernel(sums_ref, own_ref, ends_ref, out_ref):
@@ -355,42 +363,43 @@
             high = whole.astype(bf16)
             halves += [high, (whole - high.astype(f32)).astype(bf16)]
         total = jnp.dot(jnp.concatenate(halves, axis=1), ends_ref[...], preferred_element_type=f32)
-        out_ref[0, 0, iz] = own_ref[0, 0, iz] - total.T[:8]
-
-
-def own_call(sums, own):
+        out_ref[0, iz] = own_ref[0, iz] - total.T[:8]
+
+
+def own_call(sums, own, low, high):
     cells_x, cells_y, cells_z, _, slots = own.shape
     ends = np.zeros((6 * slots, slots), np.float32)
     for k in range(3):
         ends[2 * k * slots : 2 * (k + 1) * slots, k] = 1.0
     ends = jnp.asarray(ends, jnp.bfloat16)
-    block = pl.BlockSpec((1, 1, cells_z, 8, slots), lambda i, j: (i, j, 0, 0, 0))
+    block = (1, cells_z, 8, slots)
+    share = sums.size // sums.shape[0] * (high - low)
     return pl.pallas_call(
         own_kernel,
-        grid=(cells_x, cells_y),
-        out_shape=jax.ShapeDtypeStruct(own.shape, jnp.float32),
+        grid=(high - low,),
+        out_shape=jax.ShapeDtypeStruct((high - low,) + block[1:], jnp.float32),
         in_specs=[
-            pl.BlockSpec((1,) + sums.shape[1:], lambda i, j: (i * cells_y + j, 0, 0, 0, 0)),
-            block,
-            pl.BlockSpec(ends.shape, lambda i, j: (0, 0)),
+            pl.BlockSpec((1,) + sums.shape[1:], lambda i: (i + low, 0, 0, 0, 0)),
+            pl.BlockSpec(block, lambda i: (i + low, 0, 0, 0)),
+            pl.BlockSpec(ends.shape, lambda i: (0, 0)),
         ],
-        out_specs=block,
-        cost_estimate=pl.CostEstimate(
-            flops=8 * sums.size, transcendentals=0, bytes_accessed=4 * sums.size
-        ),
+        out_specs=pl.BlockSpec(block, lambda i: (i, 0, 0, 0)),
+        cost_estimate=pl.CostEstimate(flops=8 * share, transcendentals=0, bytes_accessed=4 * share),
         name="own_rows",
-    )(sums, own, ends)
-
-
-def final_kernel(own_ref, rz_ref, ry_ref, rzy_ref, rx_ref, *refs):
+    )(sums, own.reshape((-1,) + block[1:]), ends)
+
+
+def final_kernel(front_ref, back_ref, rz_ref, ry_ref, rzy_ref, rx_ref, *refs):
     *terms, forces_ref, energy_ref = refs
-    cells_x, cells_y, cells_z, _, slots = own_ref.shape
+    cells_x, cells_y, _, cells_z, slots = forces_ref.shape
+    split = front_ref.shape[0]
     for ix in range(cells_x):
         for iy in range(cells_y):
             sides_y = [m for m, at in enumerate((cells_y - 1, 0)) if iy == at]
             for iz in range(cells_z):
                 sides_z = [n for n, at in enumerate((cells_z - 1, 0)) if iz == at]
-                f = own_ref[ix, iy, iz]
+                line = ix * cells_y + iy
+                f = front_ref[line, iz] if line < split else back_ref[line - split, iz]
                 for n in sides_z:
                     f = f + rz_ref[ix, iy, n]
                 for m in sides_y:
@@ -464,7 +473,9 @@
         counts, (packed, pz, py, px, pc), rows, inside, within
     )
     rz, ry, rzy = to_sides(oz, oy, ozy, ny, nz)
-    own, rz = lax.optimization_barrier((own_call(sums, own), rz))
+    lines = cells_x * cells_y
+    split = (lines + 1) // 2
+    front, rz = lax.optimization_barrier((own_call(sums, own, 0, split), rz))
     ox = (
         ox
         + spread(rz[cells_x:], 2, cells_z)
@@ -472,18 +483,20 @@
         + spread(spread(rzy[cells_x:], 2, cells_z), 1, cells_y)
     )
     rx = moved(ox, 1, 0, 0)
+    sums, ox = lax.optimization_barrier((sums, ox))
+    back = own_call(sums, own, split, lines)
     if nz == 2 and ny == 2 and 2 <= nx <= 4:
         summed = ox[0, 0, 0, 3:4]
         terms = [moved(summed, i, 0, 0) for i in range(2, nx)]
     else:
         terms = [lax.psum(own[0, 0, 0, 3:4], AXES)]
         rz, ry, rzy, rx = (r.at[..., 3, :].set(0.0) for r in (rz, ry, rzy, rx))
-        own = own.at[..., 3, :].set(0.0)
+        front = front.at[..., 3, :].set(0.0)
     forces, energy = whole_call(
         final_kernel,
         "join_forces",
         [(cells_x, cells_y, 3, cells_z, slots), (1, slots)],
-        (own, rz, ry, rzy, rx, *terms),
+        (front, back, rz, ry, rzy, rx, *terms),
     )
     return (jnp.swapaxes(forces, 2, 3), energy[0, :1])
 

time: 83 us -> 82.9 us (level)
  Pallas kernels: 57.5 us -> 61.3 us
  starting transfers between devices: 15.9 us -> 13.4 us
  waiting for transfers between devices: 3.61 us -> 2.13 us
    pallas_call x2 -> x3, Pallas kernels: 44.5 us -> 48.4 us  [the longest x1 41.9 us: pair_call(): pl.pallas_call(pair_kernel, grid=(lines * steps,), out_shape=tuple((jax.S...]
    ppermute x10, starting transfers between devices: 15.9 us -> 13.4 us  [moved(): return lax.ppermute(block, AXES, route)]
    ppermute x10, waiting for transfers between devices: 3.61 us -> 2.13 us  [moved(): return lax.ppermute(block, AXES, route)]
  transfers between devices with their start and end apart: 10 -> 10, of which waited for: 4 -> 2; matrix products, arithmetic and copies ran while one was open for 0% -> 0% of each run, Pallas kernels for 18% -> 20%
where the time goes in v3:
time: 82.9 us; the launch traced here: 81.8 us
  Pallas kernels  61.3 us (74%)
  starting transfers between devices  13.4 us (16%)
  waiting for transfers between devices  2.13 us (3%)
  other arithmetic  2.06 us (2%)
  local copies, waits for them, and re-layouts  2.05 us (2%)
  between operations  0.83 us (1%)
    pallas_call x1, Pallas kernels, pair_call(): pl.pallas_call(pair_kernel, grid=(lines * steps,), out_shape=tuple((jax.S...  41.9 us
    ppermute x10, starting transfers between devices, moved(): return lax.ppermute(block, AXES, route)  13.4 us
    pallas_call x1, Pallas kernels, row_call(): pl.pallas_call(row_kernel, out_shape=(jax.ShapeDtypeStruct((cells_x * cel...  9.7 us
    pallas_call x2, Pallas kernels, own_call(): pl.pallas_call(own_kernel, grid=(high - low,), out_shape=jax.ShapeDtypeSt...  6.46 us
    pallas_call x2, Pallas kernels, whole_call(): pl.pallas_call(kernel, out_shape=tuple((jax.ShapeDtypeStruct(o, jnp.float...  3.24 us
    ppermute x10, waiting for transfers between devices, moved(): return lax.ppermute(block, AXES, route)  2.13 us
    unnamed x20, local copies, waits for them, and re-layouts  1.86 us
  transfers between devices with their start and end apart: 10, of which 2 were waited for; matrix products, arithmetic and copies ran while one was open for 0% of the time, Pallas kernels for 20%

profile of v3, /device:TPU:0, one launch (start us, length us, event | category | flops | bytes accessed | tf_op | source)
XLA Modules:
  0.0 81.8 jit_solution(11785638406523162361)
XLA Ops:
  0.6 1.6 %pack_cells.1 = (f32[1,4,8,8,128]{4,3,2,1,0:T(8,128)}, f32[1,4,2,8,128]{4,3,2,1,0:T(8,128)}) custom-call(s32[1,4,8]{2,1,0:T(4,128)} %counts_ref.3, f32[1,4,3,8,128]{4,3,2,1,0:T(8,128)} %bitcast.14, f32[1,4,8,128]{3,2,1,0:T(8,128)} %charges_ref.1, s32[1,4,8,128]{3,2,1,0:T(8,128)} %types_ref.1), custom_call_target="tpu_custom_call" | custom-call | tf_op jit(solution)/shard_map/pack_cells/pallas_call | solution.py:54
  2.2 0.5 collective-permute-start
  2.7 1.1 %collective-permute-done.pz_ref = f32[1,4,2,8,128]{4,3,2,1,0:T(8,128)S(1)} collective-permute-done((f32[1,4,2,8,128]{4,3,2,1,0:T(8,128)}, f32[1,4,2,8,128]{4,3,2,1,0:T(8,128)S(1)}, u32[]{:S(2)}, u32[]{:S(2)}) %collective-permute-start) | collective-permute-done | bytes 32800 | tf_op jit(solution)/shard_map/ppermute | solution.py:32
  3.8 0.9 %pad_maximum_fusion = f32[1,4,10,8,128]{4,3,2,1,0:T(8,128)S(1)} fusion(f32[1,4,1,8,128]{4,3,2,1,0:T(8,128)S(1)} %get-tuple-element.47, f32[1,4,8,8,128]{4,3,2,1,0:T(8,128)} %get-tuple-element.19.packed_ref, f32[1,4,1,8,128]{4,3,2,1,0:T(8,128)S(1)} %get-tuple-element.46), kind=kLoop, calls=%fused_computation | loop fusion | flops 81920 | bytes 327680 | tf_op jit(solution)/shard_map/concatenate | solution.py:463
  4.7 5.0 %collective-permute-start.2 = (f32[1,4,10,8,128]{4,3,2,1,0:T(8,128)S(1)}, f32[1,4,10,8,128]{4,3,2,1,0:T(8,128)S(1)}, u32[]{:S(2)}, u32[]{:S(2)}) collective-permute-start(f32[1,4,10,8,128]{4,3,2,1,0:T(8,128)S(1)} %pad_maximum_fusion), channel_id=1, source_target_pairs={{4,0},{5,1},{6,2},{7,3},{8,4},{9,5},{10,6},{11,7},{12,8},{13,9},{1... | collective-permute-start | bytes 491528 | tf_op jit(solution)/shard_map/ppermute | solution.py:32
  9.7 1.4 %collective-permute-start.3 = (f32[1,2,10,8,128]{4,3,2,1,0:T(8,128)S(1)}, f32[1,2,10,8,128]{4,3,2,1,0:T(8,128)S(1)}, u32[]{:S(2)}, u32[]{:S(2)}) collective-permute-start(f32[1,2,10,8,128]{4,3,2,1,0:T(8,128)S(1)} %pad_maximum_fusion.1), channel_id=1, source_target_pairs={{6,0},{7,1},{4,2},{5,3},{10,4},{11,5},{8,6},{9,7},{14,8},{15,9},{1... | collective-permute-start | bytes 245768 | tf_op jit(solution)/shard_map/ppermute | solution.py:32
  11.1 0.5 collective-permute-start.1
  11.6 9.7 %row_operands.1 = (f32[4,8,6,128,128]{4,3,2,1,0:T(8,128)}, f32[4,8,3,8,128]{4,3,2,1,0:T(8,128)}, f32[8,128]{1,0:T(8,128)}) custom-call(f32[1,4,8,8,128]{4,3,2,1,0:T(8,128)} %get-tuple-element.19.packed_ref, f32[64,64]{1,0:T(8,128)} %c6_ref.1, f32[64,64]{1,0:T(8,128)} %c12_ref.1, bf16[24,640]{1,0:T(8,128)(2,1)} %constant.4.clone.left_ref), custom_call_target="tpu_custom_call" | custom-call | flops 394264576 | bytes 12582912 | tf_op jit(solution)/shard_map/row_operands/pallas_call | solution.py:170
  21.3 0.0 copy-start.7
  21.3 0.0 collective-permute-done.3.pc_ref
  21.4 0.6 copy-done.7
  22.0 0.0 copy-done.5
  22.0 0.1 copy-done.1
  22.1 41.9 %pair_forces.1 = (f32[1,4,8,8,128]{4,3,2,1,0:T(8,128)}, f32[2,4,2,8,128]{4,3,2,1,0:T(8,128)}, f32[2,2,8,8,128]{4,3,2,1,0:T(8,128)}, f32[2,2,2,8,128]{4,3,2,1,0:T...) custom-call(s32[1,4,8]{2,1,0:T(4,128)} %counts_ref.3, ...), custom_call_target="tpu_custom_call" | custom-call | tf_op jit(solution)/shard_map/pair_forces/pallas_call | solution.py:338
  64.0 0.0 collective-permute-start.6
  64.0 0.1 pad.10.clone
  64.1 0.1 pad.7.clone
  64.2 0.8 %collective-permute-start.4 = (f32[2,4,2,8,128]{4,3,2,1,0:T(8,128)}, f32[2,4,2,8,128]{4,3,2,1,0:T(8,128)S(1)}, u32[]{:S(2)}, u32[]{:S(2)}) collective-permute-start(f32[2,4,2,8,128]{4,3,2,1,0:T(8,128)} %get-tuple-element.26), channel_id=1, source_target_pairs={{1,0},{0,1},{3,2},{2,3},{5,4},{4,5},{7,6},{6,7},{9,8},{8,9},{11,10... | collective-permute-start | bytes 196616 | tf_op jit(solution)/shard_map/ppermute | solution.py:32
  65.0 1.3 %collective-permute-start.5 = (f32[2,2,8,8,128]{4,3,2,1,0:T(8,128)}, f32[2,2,8,8,128]{4,3,2,1,0:T(8,128)S(1)}, u32[]{:S(2)}, u32[]{:S(2)}) collective-permute-start(f32[2,2,8,8,128]{4,3,2,1,0:T(8,128)} %get-tuple-element.30), channel_id=1, source_target_pairs={{2,0},{3,1},{0,2},{1,3},{6,4},{7,5},{4,6},{5,7},{10,8},{11,9},{8,1... | collective-permute-start | bytes 393224 | tf_op jit(solution)/shard_map/ppermute | solution.py:32
  66.3 3.2 %own_rows.2.front_ref = f32[2,8,8,128]{3,2,1,0:T(8,128)} custom-call(f32[4,8,3,128,128]{4,3,2,1,0:T(8,128)} %bitcast.9, f32[4,8,8,128]{3,2,1,0:T(8,128)} %bitcast.12, bf16[768,128]{1,0:T(8,128)(2,1)} %constant.2.clone.ends_ref), custom_call_target="tpu_custom_call" | custom-call | flops 6291456 | bytes 3145728 | tf_op jit(solution)/shard_map/own_rows/pallas_call | solution.py:377
  69.5 0.0 collective-permute-done.6.rzy_ref
  69.5 0.1 pad_maximum_fusion.2
  69.6 1.0 %collective-permute-done.5.ry_ref = f32[2,2,8,8,128]{4,3,2,1,0:T(8,128)S(1)} collective-permute-done((f32[2,2,8,8,128]{4,3,2,1,0:T(8,128)}, f32[2,2,8,8,128]{4,3,2,1,0:T(8,128)S(1)}, u32[]{:S(2)}, u32[]{:S(2)}) %collective-permute-start.5) | collective-permute-done | bytes 131104 | tf_op jit(solution)/shard_map/ppermute | solution.py:32
  70.7 1.0 %fusion.1 = f32[1,4,8,8,128]{4,3,2,1,0:T(8,128)S(1)} fusion(f32[1,4,8,8,128]{4,3,2,1,0:T(8,128)} %get-tuple-element.28, f32[1,4,1,8,128]{4,3,2,1,0:T(8,128)S(1)} %get-tuple-element.43, f32[1,4,1,8,128]{4,3,2,1,0:T(8,128)S(1)} %get-tuple-element.42, f32[1,1,8,8,128]{4,3,2,1,0:T(8,128)S(1)} %get-tuple-element.39, ...), kind=kLoop, calls=%fused_computation.3 | loop fusion | flops 294912 | bytes 426032 | tf_op jit(solution)/shard_map/add | solution.py:480
  71.8 0.4 collective-permute-start.7
  72.2 1.0 %collective-permute-start.8 = (f32[1,128]{1,0:T(1,128)S(1)}, f32[1,128]{1,0:T(1,128)S(1)}, u32[]{:S(2)}, u32[]{:S(2)}) collective-permute-start(f32[1,128]{1,0:T(1,128)S(1)} %slice_bitcast_fusion), channel_id=1, source_target_pairs={{8,0},{9,1},{10,2},{11,3},{12,4},{13,5},{14,6},{15,7},{0,8},{1,9},... | collective-permute-start | bytes 1544 | tf_op jit(solution)/shard_map/ppermute | solution.py:32
  73.2 2.5 %collective-permute-start.9 = (f32[1,128]{1,0:T(1,128)S(1)}, f32[1,128]{1,0:T(1,128)S(1)}, u32[]{:S(2)}, u32[]{:S(2)}) collective-permute-start(f32[1,128]{1,0:T(1,128)S(1)} %slice_bitcast_fusion), channel_id=1, source_target_pairs={{4,0},{5,1},{6,2},{7,3},{8,4},{9,5},{10,6},{11,7},{12,8},{13,9},{1... | collective-permute-start | bytes 1544 | tf_op jit(solution)/shard_map/ppermute | solution.py:32
  75.6 3.2 %own_rows.3.back_ref = f32[2,8,8,128]{3,2,1,0:T(8,128)} custom-call(f32[4,8,3,128,128]{4,3,2,1,0:T(8,128)} %bitcast.10, f32[4,8,8,128]{3,2,1,0:T(8,128)} %bitcast.13, bf16[768,128]{1,0:T(8,128)(2,1)} %constant.2.clone.ends_ref), custom_call_target="tpu_custom_call" | custom-call | flops 6291456 | bytes 3145728 | tf_op jit(solution)/shard_map/own_rows/pallas_call | solution.py:377
  78.9 0.5 copy-done.8
  79.4 0.1 copy-done.9
  79.5 0.6 copy-done.4
  80.1 1.7 %join_forces.1 = (f32[1,4,3,8,128]{4,3,2,1,0:T(8,128)}, f32[1,128]{1,0:T(1,128)}) custom-call(f32[2,8,8,128]{3,2,1,0:T(8,128)} %own_rows.2.front_ref, f32[2,8,8,128]{3,2,1,0:T(8,128)} %own_rows.3.back_ref, f32[2,4,2,8,128]{4,3,2,1,0:T(8,128)} %copy-done.2, f32[2,2,8,8,128]{4,3,2,1,0:T(8,128)} %copy-done, f32[2,2,2,8,128]{4,3,2,1,0:T(8,128)} %copy-done.6, ...), custom_call_target="tpu_custom_call" | custom-call | tf_op jit(solution)/shard_map/join_forces/pallas_call | solution.py:54
  (29 shorter events, 0.1 us)
Async XLA Ops:
  2.2 1.6 %collective-permute-start = (f32[1,4,2,8,128]{4,3,2,1,0:T(8,128)}, f32[1,4,2,8,128]{4,3,2,1,0:T(8,128)S(1)}, u32[]{:S(2)}, u32[]{:S(2)}) collective-permute-start(f32[1,4,2,8,128]{4,3,2,1,0:T(8,128)} %get-tuple-element.20), channel_id=1, source_target_pairs={{1,0},{0,1},{3,2},{2,3},{5,4},{4,5},{7,6},{6,7},{9,8},{8,9},{11,10... | collective-permute-start | bytes 98312 | tf_op jit(solution)/shard_map/ppermute | solution.py:32
  3.7 17.6 %copy-start.3 = (f32[1,4,2,8,128]{4,3,2,1,0:T(8,128)}, f32[1,4,2,8,128]{4,3,2,1,0:T(8,128)S(1)}, u32[]{:S(2)}) copy-start(f32[1,4,2,8,128]{4,3,2,1,0:T(8,128)S(1)} %collective-permute-done.pz_ref) | copy-start | bytes 98308
  4.7 16.7 %collective-permute-start.2 = (f32[1,4,10,8,128]{4,3,2,1,0:T(8,128)S(1)}, f32[1,4,10,8,128]{4,3,2,1,0:T(8,128)S(1)}, u32[]{:S(2)}, u32[]{:S(2)}) collective-permute-start(f32[1,4,10,8,128]{4,3,2,1,0:T(8,128)S(1)} %pad_maximum_fusion), channel_id=1, source_target_pairs={{4,0},{5,1},{6,2},{7,3},{8,4},{9,5},{10,6},{11,7},{12,8},{13,9},{1... | collective-permute-start | bytes 491528 | tf_op jit(solution)/shard_map/ppermute | solution.py:32
  9.7 11.7 %collective-permute-start.3 = (f32[1,2,10,8,128]{4,3,2,1,0:T(8,128)S(1)}, f32[1,2,10,8,128]{4,3,2,1,0:T(8,128)S(1)}, u32[]{:S(2)}, u32[]{:S(2)}) collective-permute-start(f32[1,2,10,8,128]{4,3,2,1,0:T(8,128)S(1)} %pad_maximum_fusion.1), channel_id=1, source_target_pairs={{6,0},{7,1},{4,2},{5,3},{10,4},{11,5},{8,6},{9,7},{14,8},{15,9},{1... | collective-permute-start | bytes 245768 | tf_op jit(solution)/shard_map/ppermute | solution.py:32
  11.1 10.3 %collective-permute-start.1 = (f32[1,1,10,8,128]{4,3,2,1,0:T(8,128)S(1)}, f32[1,1,10,8,128]{4,3,2,1,0:T(8,128)S(1)}, u32[]{:S(2)}, u32[]{:S(2)}) collective-permute-start(f32[1,1,10,8,128]{4,3,2,1,0:T(8,128)S(1)} %get-tuple-element.37), channel_id=1, source_target_pairs={{2,0},{3,1},{0,2},{1,3},{6,4},{7,5},{4,6},{5,7},{10,8},{11,9},{8,1... | collective-permute-start | bytes 122888 | tf_op jit(solution)/shard_map/ppermute | solution.py:32
  21.3 0.6 copy-start.7
  21.4 0.6 copy-start.5
  21.4 0.7 copy-start.1
  64.0 5.5 %collective-permute-start.6 = (f32[2,2,2,8,128]{4,3,2,1,0:T(8,128)}, f32[2,2,2,8,128]{4,3,2,1,0:T(8,128)S(1)}, u32[]{:S(2)}, u32[]{:S(2)}) collective-permute-start(f32[2,2,2,8,128]{4,3,2,1,0:T(8,128)} %get-tuple-element.31), channel_id=1, source_target_pairs={{3,0},{2,1},{1,2},{0,3},{7,4},{6,5},{5,6},{4,7},{11,8},{10,9},{9,1... | collective-permute-start | bytes 98312 | tf_op jit(solution)/shard_map/ppermute | solution.py:32
  64.2 5.5 %collective-permute-start.4 = (f32[2,4,2,8,128]{4,3,2,1,0:T(8,128)}, f32[2,4,2,8,128]{4,3,2,1,0:T(8,128)S(1)}, u32[]{:S(2)}, u32[]{:S(2)}) collective-permute-start(f32[2,4,2,8,128]{4,3,2,1,0:T(8,128)} %get-tuple-element.26), channel_id=1, source_target_pairs={{1,0},{0,1},{3,2},{2,3},{5,4},{4,5},{7,6},{6,7},{9,8},{8,9},{11,10... | collective-permute-start | bytes 196616 | tf_op jit(solution)/shard_map/ppermute | solution.py:32
  65.0 5.7 %collective-permute-start.5 = (f32[2,2,8,8,128]{4,3,2,1,0:T(8,128)}, f32[2,2,8,8,128]{4,3,2,1,0:T(8,128)S(1)}, u32[]{:S(2)}, u32[]{:S(2)}) collective-permute-start(f32[2,2,8,8,128]{4,3,2,1,0:T(8,128)} %get-tuple-element.30), channel_id=1, source_target_pairs={{2,0},{3,1},{0,2},{1,3},{6,4},{7,5},{4,6},{5,7},{10,8},{11,9},{8,1... | collective-permute-start | bytes 393224 | tf_op jit(solution)/shard_map/ppermute | solution.py:32
  69.5 9.4 %copy-start.6 = (f32[2,2,2,8,128]{4,3,2,1,0:T(8,128)}, f32[2,2,2,8,128]{4,3,2,1,0:T(8,128)S(1)}, u32[]{:S(2)}) copy-start(f32[2,2,2,8,128]{4,3,2,1,0:T(8,128)S(1)} %collective-permute-done.6.rzy_ref) | copy-start | bytes 98308
  69.6 9.3 %copy-start.2 = (f32[2,4,2,8,128]{4,3,2,1,0:T(8,128)}, f32[2,4,2,8,128]{4,3,2,1,0:T(8,128)S(1)}, u32[]{:S(2)}) copy-start(f32[2,4,2,8,128]{4,3,2,1,0:T(8,128)S(1)} %collective-permute-done.4.rz_ref) | copy-start | bytes 196612
  70.7 8.2 %copy-start = (f32[2,2,8,8,128]{4,3,2,1,0:T(8,128)}, f32[2,2,8,8,128]{4,3,2,1,0:T(8,128)S(1)}, u32[]{:S(2)}) copy-start(f32[2,2,8,8,128]{4,3,2,1,0:T(8,128)S(1)} %collective-permute-done.5.ry_ref) | copy-start | bytes 393220
  71.8 7.1 %collective-permute-start.7 = (f32[1,4,8,8,128]{4,3,2,1,0:T(8,128)S(1)}, f32[1,4,8,8,128]{4,3,2,1,0:T(8,128)S(1)}, u32[]{:S(2)}, u32[]{:S(2)}) collective-permute-start(f32[1,4,8,8,128]{4,3,2,1,0:T(8,128)S(1)} %fusion.1), channel_id=1, source_target_pairs={{12,0},{13,1},{14,2},{15,3},{0,4},{1,5},{2,6},{3,7},{4,8},{5,9},{6... | collective-permute-start | bytes 393224 | tf_op jit(solution)/shard_map/ppermute | solution.py:32
  72.2 6.7 %collective-permute-start.8 = (f32[1,128]{1,0:T(1,128)S(1)}, f32[1,128]{1,0:T(1,128)S(1)}, u32[]{:S(2)}, u32[]{:S(2)}) collective-permute-start(f32[1,128]{1,0:T(1,128)S(1)} %slice_bitcast_fusion), channel_id=1, source_target_pairs={{8,0},{9,1},{10,2},{11,3},{12,4},{13,5},{14,6},{15,7},{0,8},{1,9},... | collective-permute-start | bytes 1544 | tf_op jit(solution)/shard_map/ppermute | solution.py:32
  73.2 5.7 %collective-permute-start.9 = (f32[1,128]{1,0:T(1,128)S(1)}, f32[1,128]{1,0:T(1,128)S(1)}, u32[]{:S(2)}, u32[]{:S(2)}) collective-permute-start(f32[1,128]{1,0:T(1,128)S(1)} %slice_bitcast_fusion), channel_id=1, source_target_pairs={{4,0},{5,1},{6,2},{7,3},{8,4},{9,5},{10,6},{11,7},{12,8},{13,9},{1... | collective-permute-start | bytes 1544 | tf_op jit(solution)/shard_map/ppermute | solution.py:32
  78.9 0.5 copy-start.8
  78.9 0.6 copy-start.9
  79.5 0.6 copy-start.4

commit v4 on v3

--- a/solution.py
+++ b/solution.py
@@ -149,7 +149,7 @@
                 self_ref[line, iz, k] = fold[k]
             return energy
 
-        return lax.fori_loop(0, cells_z, inside, energy)
+        return lax.fori_loop(0, cells_z, inside, energy, unroll=2 if cells_z % 2 == 0 else 1)
 
     energy = lax.fori_loop(0, lines, do_line, jnp.zeros((8, slots), f32))
     energy_ref[...] = 0.5 * energy

time: 82.9 us -> 82.3 us (level)
  Pallas kernels: 61.3 us -> 60.4 us
  transfers between devices with their start and end apart: 10 -> 10, of which waited for: 2 -> 2; matrix products, arithmetic and copies ran while one was open for 0% -> 0% of each run, Pallas kernels for 20% -> 19%
where the time goes in v4:
time: 82.3 us; the launch traced here: 82 us
  Pallas kernels  60.4 us (73%)
  starting transfers between devices  13.8 us (17%)
  waiting for transfers between devices  2.84 us (3%)
  other arithmetic  2.06 us (3%)
  local copies, waits for them, and re-layouts  2.05 us (2%)
  between operations  0.83 us (1%)
    pallas_call x1, Pallas kernels, pair_call(): pl.pallas_call(pair_kernel, grid=(lines * steps,), out_shape=tuple((jax.S...  41.6 us
    ppermute x10, starting transfers between devices, moved(): return lax.ppermute(block, AXES, route)  13.8 us
    pallas_call x1, Pallas kernels, row_call(): pl.pallas_call(row_kernel, out_shape=(jax.ShapeDtypeStruct((cells_x * cel...  9.01 us
    pallas_call x2, Pallas kernels, own_call(): pl.pallas_call(own_kernel, grid=(high - low,), out_shape=jax.ShapeDtypeSt...  6.46 us
    pallas_call x2, Pallas kernels, whole_call(): pl.pallas_call(kernel, out_shape=tuple((jax.ShapeDtypeStruct(o, jnp.float...  3.24 us
    ppermute x10, waiting for transfers between devices, moved(): return lax.ppermute(block, AXES, route)  2.84 us
    unnamed x20, local copies, waits for them, and re-layouts  1.86 us
  transfers between devices with their start and end apart: 10, of which 2 were waited for; matrix products, arithmetic and copies ran while one was open for 0% of the time, Pallas kernels for 19%

profile of v4, /device:TPU:0, one launch (start us, length us, event | category | flops | bytes accessed | tf_op | source)
XLA Modules:
  0.0 82.0 jit_solution(4704247114025339169)
XLA Ops:
  0.6 1.6 %pack_cells.1 = (f32[1,4,8,8,128]{4,3,2,1,0:T(8,128)}, f32[1,4,2,8,128]{4,3,2,1,0:T(8,128)}) custom-call(s32[1,4,8]{2,1,0:T(4,128)} %counts_ref.3, f32[1,4,3,8,128]{4,3,2,1,0:T(8,128)} %bitcast.14, f32[1,4,8,128]{3,2,1,0:T(8,128)} %charges_ref.1, s32[1,4,8,128]{3,2,1,0:T(8,128)} %types_ref.1), custom_call_target="tpu_custom_call" | custom-call | tf_op jit(solution)/shard_map/pack_cells/pallas_call | solution.py:54
  2.2 0.5 collective-permute-start
  2.7 1.1 %collective-permute-done.pz_ref = f32[1,4,2,8,128]{4,3,2,1,0:T(8,128)S(1)} collective-permute-done((f32[1,4,2,8,128]{4,3,2,1,0:T(8,128)}, f32[1,4,2,8,128]{4,3,2,1,0:T(8,128)S(1)}, u32[]{:S(2)}, u32[]{:S(2)}) %collective-permute-start) | collective-permute-done | bytes 32800 | tf_op jit(solution)/shard_map/ppermute | solution.py:32
  3.8 0.9 %pad_maximum_fusion = f32[1,4,10,8,128]{4,3,2,1,0:T(8,128)S(1)} fusion(f32[1,4,1,8,128]{4,3,2,1,0:T(8,128)S(1)} %get-tuple-element.47, f32[1,4,8,8,128]{4,3,2,1,0:T(8,128)} %get-tuple-element.19.packed_ref, f32[1,4,1,8,128]{4,3,2,1,0:T(8,128)S(1)} %get-tuple-element.46), kind=kLoop, calls=%fused_computation | loop fusion | flops 81920 | bytes 327680 | tf_op jit(solution)/shard_map/concatenate | solution.py:463
  4.7 5.0 %collective-permute-start.2 = (f32[1,4,10,8,128]{4,3,2,1,0:T(8,128)S(1)}, f32[1,4,10,8,128]{4,3,2,1,0:T(8,128)S(1)}, u32[]{:S(2)}, u32[]{:S(2)}) collective-permute-start(f32[1,4,10,8,128]{4,3,2,1,0:T(8,128)S(1)} %pad_maximum_fusion), channel_id=1, source_target_pairs={{4,0},{5,1},{6,2},{7,3},{8,4},{9,5},{10,6},{11,7},{12,8},{13,9},{1... | collective-permute-start | bytes 491528 | tf_op jit(solution)/shard_map/ppermute | solution.py:32
  9.7 1.4 %collective-permute-start.3 = (f32[1,2,10,8,128]{4,3,2,1,0:T(8,128)S(1)}, f32[1,2,10,8,128]{4,3,2,1,0:T(8,128)S(1)}, u32[]{:S(2)}, u32[]{:S(2)}) collective-permute-start(f32[1,2,10,8,128]{4,3,2,1,0:T(8,128)S(1)} %pad_maximum_fusion.1), channel_id=1, source_target_pairs={{6,0},{7,1},{4,2},{5,3},{10,4},{11,5},{8,6},{9,7},{14,8},{15,9},{1... | collective-permute-start | bytes 245768 | tf_op jit(solution)/shard_map/ppermute | solution.py:32
  11.1 0.5 collective-permute-start.1
  11.6 9.0 %row_operands.1 = (f32[4,8,6,128,128]{4,3,2,1,0:T(8,128)}, f32[4,8,3,8,128]{4,3,2,1,0:T(8,128)}, f32[8,128]{1,0:T(8,128)}) custom-call(f32[1,4,8,8,128]{4,3,2,1,0:T(8,128)} %get-tuple-element.19.packed_ref, f32[64,64]{1,0:T(8,128)} %c6_ref.1, f32[64,64]{1,0:T(8,128)} %c12_ref.1, bf16[24,640]{1,0:T(8,128)(2,1)} %constant.4.clone.left_ref), custom_call_target="tpu_custom_call" | custom-call | flops 394264576 | bytes 12582912 | tf_op jit(solution)/shard_map/row_operands/pallas_call | solution.py:170
  20.6 0.0 copy-start.7
  20.7 0.0 collective-permute-done.3.pc_ref
  20.7 0.0 collective-permute-done.2.px_ref
  20.7 0.6 copy-done.7
  21.3 0.0 copy-done.5
  21.3 0.1 copy-done.1
  21.4 41.6 %pair_forces.1 = (f32[1,4,8,8,128]{4,3,2,1,0:T(8,128)}, f32[2,4,2,8,128]{4,3,2,1,0:T(8,128)}, f32[2,2,8,8,128]{4,3,2,1,0:T(8,128)}, f32[2,2,2,8,128]{4,3,2,1,0:T...) custom-call(s32[1,4,8]{2,1,0:T(4,128)} %counts_ref.3, ...), custom_call_target="tpu_custom_call" | custom-call | tf_op jit(solution)/shard_map/pair_forces/pallas_call | solution.py:338
  63.0 0.0 collective-permute-start.6
  63.0 0.1 pad.10.clone
  63.1 0.1 pad.7.clone
  63.2 1.6 %collective-permute-start.4 = (f32[2,4,2,8,128]{4,3,2,1,0:T(8,128)}, f32[2,4,2,8,128]{4,3,2,1,0:T(8,128)S(1)}, u32[]{:S(2)}, u32[]{:S(2)}) collective-permute-start(f32[2,4,2,8,128]{4,3,2,1,0:T(8,128)} %get-tuple-element.26), channel_id=1, source_target_pairs={{1,0},{0,1},{3,2},{2,3},{5,4},{4,5},{7,6},{6,7},{9,8},{8,9},{11,10... | collective-permute-start | bytes 196616 | tf_op jit(solution)/shard_map/ppermute | solution.py:32
  64.7 0.6 collective-permute-start.5
  65.3 3.2 %own_rows.2.front_ref = f32[2,8,8,128]{3,2,1,0:T(8,128)} custom-call(f32[4,8,3,128,128]{4,3,2,1,0:T(8,128)} %bitcast.9, f32[4,8,8,128]{3,2,1,0:T(8,128)} %bitcast.12, bf16[768,128]{1,0:T(8,128)(2,1)} %constant.2.clone.ends_ref), custom_call_target="tpu_custom_call" | custom-call | flops 6291456 | bytes 3145728 | tf_op jit(solution)/shard_map/own_rows/pallas_call | solution.py:377
  68.5 0.0 collective-permute-done.6.rzy_ref
  68.6 0.1 pad_maximum_fusion.2
  68.7 1.8 %collective-permute-done.5.ry_ref = f32[2,2,8,8,128]{4,3,2,1,0:T(8,128)S(1)} collective-permute-done((f32[2,2,8,8,128]{4,3,2,1,0:T(8,128)}, f32[2,2,8,8,128]{4,3,2,1,0:T(8,128)S(1)}, u32[]{:S(2)}, u32[]{:S(2)}) %collective-permute-start.5) | collective-permute-done | bytes 131104 | tf_op jit(solution)/shard_map/ppermute | solution.py:32
  70.4 1.0 %fusion.1 = f32[1,4,8,8,128]{4,3,2,1,0:T(8,128)S(1)} fusion(f32[1,4,8,8,128]{4,3,2,1,0:T(8,128)} %get-tuple-element.28, f32[1,4,1,8,128]{4,3,2,1,0:T(8,128)S(1)} %get-tuple-element.43, f32[1,4,1,8,128]{4,3,2,1,0:T(8,128)S(1)} %get-tuple-element.42, f32[1,1,8,8,128]{4,3,2,1,0:T(8,128)S(1)} %get-tuple-element.39, ...), kind=kLoop, calls=%fused_computation.3 | loop fusion | flops 294912 | bytes 426032 | tf_op jit(solution)/shard_map/add | solution.py:480
  71.5 1.9 %collective-permute-start.7 = (f32[1,4,8,8,128]{4,3,2,1,0:T(8,128)S(1)}, f32[1,4,8,8,128]{4,3,2,1,0:T(8,128)S(1)}, u32[]{:S(2)}, u32[]{:S(2)}) collective-permute-start(f32[1,4,8,8,128]{4,3,2,1,0:T(8,128)S(1)} %fusion.1), channel_id=1, source_target_pairs={{12,0},{13,1},{14,2},{15,3},{0,4},{1,5},{2,6},{3,7},{4,8},{5,9},{6... | collective-permute-start | bytes 393224 | tf_op jit(solution)/shard_map/ppermute | solution.py:32
  73.4 2.4 %collective-permute-start.9 = (f32[1,128]{1,0:T(1,128)S(1)}, f32[1,128]{1,0:T(1,128)S(1)}, u32[]{:S(2)}, u32[]{:S(2)}) collective-permute-start(f32[1,128]{1,0:T(1,128)S(1)} %slice_bitcast_fusion), channel_id=1, source_target_pairs={{4,0},{5,1},{6,2},{7,3},{8,4},{9,5},{10,6},{11,7},{12,8},{13,9},{1... | collective-permute-start | bytes 1544 | tf_op jit(solution)/shard_map/ppermute | solution.py:32
  75.8 3.2 %own_rows.3.back_ref = f32[2,8,8,128]{3,2,1,0:T(8,128)} custom-call(f32[4,8,3,128,128]{4,3,2,1,0:T(8,128)} %bitcast.10, f32[4,8,8,128]{3,2,1,0:T(8,128)} %bitcast.13, bf16[768,128]{1,0:T(8,128)(2,1)} %constant.2.clone.ends_ref), custom_call_target="tpu_custom_call" | custom-call | flops 6291456 | bytes 3145728 | tf_op jit(solution)/shard_map/own_rows/pallas_call | solution.py:377
  79.1 0.5 copy-done.8
  79.6 0.1 copy-done.9
  79.7 0.6 copy-done.4
  80.3 1.7 %join_forces.1 = (f32[1,4,3,8,128]{4,3,2,1,0:T(8,128)}, f32[1,128]{1,0:T(1,128)}) custom-call(f32[2,8,8,128]{3,2,1,0:T(8,128)} %own_rows.2.front_ref, f32[2,8,8,128]{3,2,1,0:T(8,128)} %own_rows.3.back_ref, f32[2,4,2,8,128]{4,3,2,1,0:T(8,128)} %copy-done.2, f32[2,2,8,8,128]{4,3,2,1,0:T(8,128)} %copy-done, f32[2,2,2,8,128]{4,3,2,1,0:T(8,128)} %copy-done.6, ...), custom_call_target="tpu_custom_call" | custom-call | tf_op jit(solution)/shard_map/join_forces/pallas_call | solution.py:54
  (29 shorter events, 0.1 us)
Async XLA Ops:
  2.2 1.6 %collective-permute-start = (f32[1,4,2,8,128]{4,3,2,1,0:T(8,128)}, f32[1,4,2,8,128]{4,3,2,1,0:T(8,128)S(1)}, u32[]{:S(2)}, u32[]{:S(2)}) collective-permute-start(f32[1,4,2,8,128]{4,3,2,1,0:T(8,128)} %get-tuple-element.20), channel_id=1, source_target_pairs={{1,0},{0,1},{3,2},{2,3},{5,4},{4,5},{7,6},{6,7},{9,8},{8,9},{11,10... | collective-permute-start | bytes 98312 | tf_op jit(solution)/shard_map/ppermute | solution.py:32
  3.7 16.9 %copy-start.3 = (f32[1,4,2,8,128]{4,3,2,1,0:T(8,128)}, f32[1,4,2,8,128]{4,3,2,1,0:T(8,128)S(1)}, u32[]{:S(2)}) copy-start(f32[1,4,2,8,128]{4,3,2,1,0:T(8,128)S(1)} %collective-permute-done.pz_ref) | copy-start | bytes 98308
  4.7 16.0 %collective-permute-start.2 = (f32[1,4,10,8,128]{4,3,2,1,0:T(8,128)S(1)}, f32[1,4,10,8,128]{4,3,2,1,0:T(8,128)S(1)}, u32[]{:S(2)}, u32[]{:S(2)}) collective-permute-start(f32[1,4,10,8,128]{4,3,2,1,0:T(8,128)S(1)} %pad_maximum_fusion), channel_id=1, source_target_pairs={{4,0},{5,1},{6,2},{7,3},{8,4},{9,5},{10,6},{11,7},{12,8},{13,9},{1... | collective-permute-start | bytes 491528 | tf_op jit(solution)/shard_map/ppermute | solution.py:32
  9.7 11.0 %collective-permute-start.3 = (f32[1,2,10,8,128]{4,3,2,1,0:T(8,128)S(1)}, f32[1,2,10,8,128]{4,3,2,1,0:T(8,128)S(1)}, u32[]{:S(2)}, u32[]{:S(2)}) collective-permute-start(f32[1,2,10,8,128]{4,3,2,1,0:T(8,128)S(1)} %pad_maximum_fusion.1), channel_id=1, source_target_pairs={{6,0},{7,1},{4,2},{5,3},{10,4},{11,5},{8,6},{9,7},{14,8},{15,9},{1... | collective-permute-start | bytes 245768 | tf_op jit(solution)/shard_map/ppermute | solution.py:32
  11.1 9.6 %collective-permute-start.1 = (f32[1,1,10,8,128]{4,3,2,1,0:T(8,128)S(1)}, f32[1,1,10,8,128]{4,3,2,1,0:T(8,128)S(1)}, u32[]{:S(2)}, u32[]{:S(2)}) collective-permute-start(f32[1,1,10,8,128]{4,3,2,1,0:T(8,128)S(1)} %get-tuple-element.37), channel_id=1, source_target_pairs={{2,0},{3,1},{0,2},{1,3},{6,4},{7,5},{4,6},{5,7},{10,8},{11,9},{8,1... | collective-permute-start | bytes 122888 | tf_op jit(solution)/shard_map/ppermute | solution.py:32
  20.6 0.6 copy-start.7
  20.7 0.6 copy-start.5
  20.7 0.7 copy-start.1
  63.0 5.5 %collective-permute-start.6 = (f32[2,2,2,8,128]{4,3,2,1,0:T(8,128)}, f32[2,2,2,8,128]{4,3,2,1,0:T(8,128)S(1)}, u32[]{:S(2)}, u32[]{:S(2)}) collective-permute-start(f32[2,2,2,8,128]{4,3,2,1,0:T(8,128)} %get-tuple-element.31), channel_id=1, source_target_pairs={{3,0},{2,1},{1,2},{0,3},{7,4},{6,5},{5,6},{4,7},{11,8},{10,9},{9,1... | collective-permute-start | bytes 98312 | tf_op jit(solution)/shard_map/ppermute | solution.py:32
  63.2 5.5 %collective-permute-start.4 = (f32[2,4,2,8,128]{4,3,2,1,0:T(8,128)}, f32[2,4,2,8,128]{4,3,2,1,0:T(8,128)S(1)}, u32[]{:S(2)}, u32[]{:S(2)}) collective-permute-start(f32[2,4,2,8,128]{4,3,2,1,0:T(8,128)} %get-tuple-element.26), channel_id=1, source_target_pairs={{1,0},{0,1},{3,2},{2,3},{5,4},{4,5},{7,6},{6,7},{9,8},{8,9},{11,10... | collective-permute-start | bytes 196616 | tf_op jit(solution)/shard_map/ppermute | solution.py:32
  64.7 5.7 %collective-permute-start.5 = (f32[2,2,8,8,128]{4,3,2,1,0:T(8,128)}, f32[2,2,8,8,128]{4,3,2,1,0:T(8,128)S(1)}, u32[]{:S(2)}, u32[]{:S(2)}) collective-permute-start(f32[2,2,8,8,128]{4,3,2,1,0:T(8,128)} %get-tuple-element.30), channel_id=1, source_target_pairs={{2,0},{3,1},{0,2},{1,3},{6,4},{7,5},{4,6},{5,7},{10,8},{11,9},{8,1... | collective-permute-start | bytes 393224 | tf_op jit(solution)/shard_map/ppermute | solution.py:32
  68.5 10.6 %copy-start.6 = (f32[2,2,2,8,128]{4,3,2,1,0:T(8,128)}, f32[2,2,2,8,128]{4,3,2,1,0:T(8,128)S(1)}, u32[]{:S(2)}) copy-start(f32[2,2,2,8,128]{4,3,2,1,0:T(8,128)S(1)} %collective-permute-done.6.rzy_ref) | copy-start | bytes 98308
  68.7 10.4 %copy-start.2 = (f32[2,4,2,8,128]{4,3,2,1,0:T(8,128)}, f32[2,4,2,8,128]{4,3,2,1,0:T(8,128)S(1)}, u32[]{:S(2)}) copy-start(f32[2,4,2,8,128]{4,3,2,1,0:T(8,128)S(1)} %collective-permute-done.4.rz_ref) | copy-start | bytes 196612
  70.4 8.7 %copy-start = (f32[2,2,8,8,128]{4,3,2,1,0:T(8,128)}, f32[2,2,8,8,128]{4,3,2,1,0:T(8,128)S(1)}, u32[]{:S(2)}) copy-start(f32[2,2,8,8,128]{4,3,2,1,0:T(8,128)S(1)} %collective-permute-done.5.ry_ref) | copy-start | bytes 393220
  71.5 7.6 %collective-permute-start.7 = (f32[1,4,8,8,128]{4,3,2,1,0:T(8,128)S(1)}, f32[1,4,8,8,128]{4,3,2,1,0:T(8,128)S(1)}, u32[]{:S(2)}, u32[]{:S(2)}) collective-permute-start(f32[1,4,8,8,128]{4,3,2,1,0:T(8,128)S(1)} %fusion.1), channel_id=1, source_target_pairs={{12,0},{13,1},{14,2},{15,3},{0,4},{1,5},{2,6},{3,7},{4,8},{5,9},{6... | collective-permute-start | bytes 393224 | tf_op jit(solution)/shard_map/ppermute | solution.py:32
  73.4 5.7 %collective-permute-start.8 = (f32[1,128]{1,0:T(1,128)S(1)}, f32[1,128]{1,0:T(1,128)S(1)}, u32[]{:S(2)}, u32[]{:S(2)}) collective-permute-start(f32[1,128]{1,0:T(1,128)S(1)} %slice_bitcast_fusion), channel_id=1, source_target_pairs={{8,0},{9,1},{10,2},{11,3},{12,4},{13,5},{14,6},{15,7},{0,8},{1,9},... | collective-permute-start | bytes 1544 | tf_op jit(solution)/shard_map/ppermute | solution.py:32
  73.4 5.7 %collective-permute-start.9 = (f32[1,128]{1,0:T(1,128)S(1)}, f32[1,128]{1,0:T(1,128)S(1)}, u32[]{:S(2)}, u32[]{:S(2)}) collective-permute-start(f32[1,128]{1,0:T(1,128)S(1)} %slice_bitcast_fusion), channel_id=1, source_target_pairs={{4,0},{5,1},{6,2},{7,3},{8,4},{9,5},{10,6},{11,7},{12,8},{13,9},{1... | collective-permute-start | bytes 1544 | tf_op jit(solution)/shard_map/ppermute | solution.py:32
  79.1 0.5 copy-start.8
  79.1 0.6 copy-start.9
  79.6 0.6 copy-start.4
